TPU v7x, 256 devices: a whole 4x4x8 slice. The times are simulated.
256 devices in a mesh: ang: 32 (over y, z_lo, core), sl: 8 (over z_hi, x).
Axes of the slice: x: 4, y: 4, z: 8 (z_hi: 2, z_lo: 4; z = z_hi * 4 + z_lo), core: 2. Of those that a mesh axis runs over, the one named last changes fastest.
Arguments:
- sinogram: bfloat16 [64, 64, 1024], P('sl', 'ang'), may hold values from -72 to 72
- detector_coord: int32 [64, 64, 512], P('ang', 'sl'), may hold values from 0 to 1072693247
Outputs:
- image_rows: float32 [64, 64, 512], P('ang', 'sl')
All inputs are finite; a program needn't handle non-finite values.
Results may differ from a plain program's by a relative error of at most 0.0052.
Values may be sent and summed in bfloat16 or wider, within the bound.
A program may use at most 64 MiB of HBM per device.

v0:
```python
import math

import jax
import jax.numpy as jnp
from jax import lax
from jax.sharding import PartitionSpec as P


def sent_to_all(array, axis):
    devices = lax.axis_size(axis)
    return lax.all_to_all(
        jnp.broadcast_to(array[None], (devices, *array.shape)), axis, 0, 0, tiled=True
    )


def in_order(tiles, dim):
    tiles = jnp.moveaxis(tiles, 0, dim)
    shape = tiles.shape
    return tiles.reshape(*shape[:dim], shape[dim] * shape[dim + 1], *shape[dim + 2 :])


def gathered_copies(array, axis, dim):
    tiles = sent_to_all(array, axis)
    return in_order(tiles, dim)


def ramp_table(bin_count):
    first = lax.broadcasted_iota(jnp.int32, (bin_count, bin_count), 0)
    second = lax.broadcasted_iota(jnp.int32, (bin_count, bin_count), 1)
    offset = second - first
    offset_sq = jnp.maximum((offset * offset).astype(jnp.float32), jnp.float32(1.0))
    odd_mask = offset % 2 != 0
    values = jnp.where(
        offset == 0,
        jnp.float32(0.25),
        jnp.where(odd_mask, jnp.float32(-1.0 / math.pi**2) / offset_sq, jnp.float32(0.0)),
    )
    return values.astype(jnp.bfloat16)


def dense_weights(row_coords, bin_count):
    bin_left = row_coords // 1048576
    fraction = (row_coords % 1048576).astype(jnp.float32) / jnp.float32(1048576.0)
    positions = lax.broadcasted_iota(jnp.int32, row_coords.shape + (bin_count,), row_coords.ndim)
    left_part = jnp.where(
        positions == bin_left[..., None], 1.0 - fraction[..., None], jnp.float32(0.0)
    )
    right_part = jnp.where(
        positions == bin_left[..., None] + 1, fraction[..., None], jnp.float32(0.0)
    )
    return (left_part + right_part).astype(jnp.bfloat16)


def project_block(coords_block, projections):
    weights = dense_weights(coords_block, projections.shape[2])
    return jnp.einsum("arxb,sab->rsx", weights, projections, preferred_element_type=jnp.float32)


def shards(sinogram, detector_coord):
    slices, angles, bin_count = sinogram.shape
    width_pixels = detector_coord.shape[2]
    table = ramp_table(bin_count)
    filtered = jnp.dot(
        sinogram.reshape(slices * angles, bin_count), table, preferred_element_type=jnp.float32
    )
    filtered = filtered.astype(jnp.bfloat16).reshape(slices, angles, bin_count)
    fbp_scale = jnp.float32(math.pi / (angles * lax.axis_size("ang")))
    coord_table = gathered_copies(detector_coord, "sl", 1)
    row_share = coord_table.shape[1] // lax.axis_size("ang")
    own_rows = lax.all_to_all(coord_table, "ang", split_axis=1, concat_axis=0, tiled=True)
    start_value = jnp.zeros((row_share, slices, width_pixels), jnp.float32)
    shard_piece = gathered_copies(filtered, "ang", 1)
    group_count = shard_piece.shape[1] // angles

    def one_group(group_step, inner):
        coords_block = lax.dynamic_slice_in_dim(own_rows, group_step * angles, angles, 0)
        projections = lax.dynamic_slice_in_dim(shard_piece, group_step * angles, angles, 1)
        return inner + project_block(coords_block, projections)

    summed = lax.fori_loop(0, group_count, one_group, start_value)
    image_rows = summed * fbp_scale
    return image_rows


def solution(mesh):
    in_specs = (P("sl", "ang", None), P("ang", "sl", None))
    out_specs = P("ang", "sl", None)
    return jax.shard_map(shards, mesh=mesh, in_specs=in_specs, out_specs=out_specs, check_vma=False)
```

profile of v0, /device:TPU:1, one launch (start us, length us, event | category | flops | bytes accessed | tf_op | source)
XLA Modules:
  0.0 153.6 jit_solution(7158897896248793487)
XLA Ops:
  0.0 1.5 broadcast_in_dim.84
  1.5 11.5 %all-to-all-start.1 = ((s32[8,2,8,512]{3,2,1,0:T(8,128)}), s32[8,2,8,512]{3,2,1,0:T(8,128)S(1)}, u32[]{:S(2)}, u32[]{:S(2)}) async-start(s32[8,2,8,512]{3,2,1,0:T(8,128)} %broadcast_in_dim.84), calls=%async_computation.1 | async-start | bytes 524288 | tf_op jit(solution)/shard_map/all_to_all | solution.py:11
  12.9 0.8 reshape.17
  13.7 9.3 %all-to-all-done.1 = s32[8,2,8,512]{3,2,1,0:T(8,128)S(1)} async-done(((s32[8,2,8,512]{3,2,1,0:T(8,128)}), s32[8,2,8,512]{3,2,1,0:T(8,128)S(1)}, u32[]{:S(2)}, u32[]{:S(2)}) %all-to-all-start.1) | async-done | bytes 262176 | tf_op jit(solution)/shard_map/all_to_all | solution.py:11
  23.0 0.9 copy.12
  23.9 10.3 %all-to-all-start.2 = ((s32[2,64,512]{2,0,1:T(2,128)}), s32[2,64,512]{2,0,1:T(2,128)S(1)}, u32[]{:S(2)}, u32[]{:S(2)}) async-start(s32[2,64,512]{2,0,1:T(2,128)} %copy.12), calls=%async_computation.2 | async-start | bytes 524288 | tf_op jit(solution)/shard_map/all_to_all | solution.py:70
  34.3 3.2 %fusion.17 = bf16[16,1024]{1,0:T(8,128)(2,1)S(1)} fusion(bf16[16,1024]{1,0:T(8,128)(2,1)S(1)} %reshape.17), kind=kOutput, calls=%fused_computation.35 | convolution fusion | flops 55590912 | bytes 65536 | tf_op jit(solution)/shard_map/dot_general | solution.py:63
  37.5 8.0 %all-to-all-done.2 = s32[2,64,512]{2,0,1:T(2,128)S(1)} async-done(((s32[2,64,512]{2,0,1:T(2,128)}), s32[2,64,512]{2,0,1:T(2,128)S(1)}, u32[]{:S(2)}, u32[]{:S(2)}) %all-to-all-start.2) | async-done | bytes 262176 | tf_op jit(solution)/shard_map/all_to_all | solution.py:70
  45.5 1.1 broadcast_in_dim.83
  46.6 3.7 %all-to-all-start = ((bf16[32,8,2,1024]{3,1,2,0:T(8,128)(2,1)}), bf16[32,8,2,1024]{3,1,2,0:T(8,128)(2,1)S(1)}, u32[]{:S(2)}, u32[]{:S(2)}) async-start(bf16[32,8,2,1024]{3,1,2,0:T(8,128)(2,1)} %broadcast_in_dim.83), calls=%async_computation | async-start | bytes 2097152 | tf_op jit(solution)/shard_map/all_to_all | solution.py:11
  50.4 0.1 copy.13
  50.5 27.6 %all-to-all-done = bf16[32,8,2,1024]{3,1,2,0:T(8,128)(2,1)S(1)} async-done(((bf16[32,8,2,1024]{3,1,2,0:T(8,128)(2,1)}), bf16[32,8,2,1024]{3,1,2,0:T(8,128)(2,1)S(1)}, u32[]{:S(2)}, u32[]{:S(2)}) %all-to-all-start) | async-done | bytes 1048608 | tf_op jit(solution)/shard_map/all_to_all | solution.py:11
  78.1 74.9 %while.16 = (s32[]{:T(128)}, f32[2,8,512]{2,1,0:T(8,128)S(1)}, bf16[8,64,1024]{2,0,1:T(8,128)(2,1)S(1)}, s32[64,2,512]{2,1,0:T(2,128)S(1)}, s32[]{:T(128)}, /*index=5*/s32[]{:T(128)}, s32[]{:T(128)}, s32[]{:T(128)}) while((s32[]{:T(128)}, f32[2,8,512]{2,1,0:T(8,128)S(1)}, bf16[8,64,1024]{2,0,1:T(8,128)(2,1)S(1)}, ...), condition=%wide.region_1.2_spmd.clone, body=%wide.region_0.1_spmd.clone.sunk | while | flops 46215176 | bytes 196757 | solution.py:80
  78.1 2.3 %fusion.30 = f32[2,8,512]{2,1,0:T(8,128)S(1)} fusion(f32[2,2,512]{2,0,1:T(2,128)S(1)} %get-tuple-element.183, s32[2,2,512]{2,0,1:T(2,128)S(1)} %get-tuple-element.184, f32[2,2,512]{2,0,1:T(2,128)S(1)} %get-tuple-element.185, s32[2,2,512]{2,0,1:T(2,128)S(1)} %get-tuple-element.186, f32[2,8,512]{2,1,0:T(8,128)S(1)} %get-tuple-element.196, ...), kind=kOutput, calls=%fused_computation.5.clone.1 | convolution fusion | flops 46153728 | bytes 131077 | tf_op jit(solution)/shard_map/while/body/eval_jaxpr/arxb,sab->rsx/dot_general | solution.py:56
  80.5 2.3 %fusion.30 = f32[2,8,512]{2,1,0:T(8,128)S(1)} fusion(f32[2,2,512]{2,0,1:T(2,128)S(1)} %get-tuple-element.183, s32[2,2,512]{2,0,1:T(2,128)S(1)} %get-tuple-element.184, f32[2,2,512]{2,0,1:T(2,128)S(1)} %get-tuple-element.185, s32[2,2,512]{2,0,1:T(2,128)S(1)} %get-tuple-element.186, f32[2,8,512]{2,1,0:T(8,128)S(1)} %get-tuple-element.196, ...), kind=kOutput, calls=%fused_computation.5.clone.1 | convolution fusion | flops 46153728 | bytes 131077 | tf_op jit(solution)/shard_map/while/body/eval_jaxpr/arxb,sab->rsx/dot_general | solution.py:56
  82.8 2.3 %fusion.30 = f32[2,8,512]{2,1,0:T(8,128)S(1)} fusion(f32[2,2,512]{2,0,1:T(2,128)S(1)} %get-tuple-element.183, s32[2,2,512]{2,0,1:T(2,128)S(1)} %get-tuple-element.184, f32[2,2,512]{2,0,1:T(2,128)S(1)} %get-tuple-element.185, s32[2,2,512]{2,0,1:T(2,128)S(1)} %get-tuple-element.186, f32[2,8,512]{2,1,0:T(8,128)S(1)} %get-tuple-element.196, ...), kind=kOutput, calls=%fused_computation.5.clone.1 | convolution fusion | flops 46153728 | bytes 131077 | tf_op jit(solution)/shard_map/while/body/eval_jaxpr/arxb,sab->rsx/dot_general | solution.py:56
  85.2 2.3 %fusion.30 = f32[2,8,512]{2,1,0:T(8,128)S(1)} fusion(f32[2,2,512]{2,0,1:T(2,128)S(1)} %get-tuple-element.183, s32[2,2,512]{2,0,1:T(2,128)S(1)} %get-tuple-element.184, f32[2,2,512]{2,0,1:T(2,128)S(1)} %get-tuple-element.185, s32[2,2,512]{2,0,1:T(2,128)S(1)} %get-tuple-element.186, f32[2,8,512]{2,1,0:T(8,128)S(1)} %get-tuple-element.196, ...), kind=kOutput, calls=%fused_computation.5.clone.1 | convolution fusion | flops 46153728 | bytes 131077 | tf_op jit(solution)/shard_map/while/body/eval_jaxpr/arxb,sab->rsx/dot_general | solution.py:56
  87.5 2.3 %fusion.30 = f32[2,8,512]{2,1,0:T(8,128)S(1)} fusion(f32[2,2,512]{2,0,1:T(2,128)S(1)} %get-tuple-element.183, s32[2,2,512]{2,0,1:T(2,128)S(1)} %get-tuple-element.184, f32[2,2,512]{2,0,1:T(2,128)S(1)} %get-tuple-element.185, s32[2,2,512]{2,0,1:T(2,128)S(1)} %get-tuple-element.186, f32[2,8,512]{2,1,0:T(8,128)S(1)} %get-tuple-element.196, ...), kind=kOutput, calls=%fused_computation.5.clone.1 | convolution fusion | flops 46153728 | bytes 131077 | tf_op jit(solution)/shard_map/while/body/eval_jaxpr/arxb,sab->rsx/dot_general | solution.py:56
  89.8 2.3 %fusion.30 = f32[2,8,512]{2,1,0:T(8,128)S(1)} fusion(f32[2,2,512]{2,0,1:T(2,128)S(1)} %get-tuple-element.183, s32[2,2,512]{2,0,1:T(2,128)S(1)} %get-tuple-element.184, f32[2,2,512]{2,0,1:T(2,128)S(1)} %get-tuple-element.185, s32[2,2,512]{2,0,1:T(2,128)S(1)} %get-tuple-element.186, f32[2,8,512]{2,1,0:T(8,128)S(1)} %get-tuple-element.196, ...), kind=kOutput, calls=%fused_computation.5.clone.1 | convolution fusion | flops 46153728 | bytes 131077 | tf_op jit(solution)/shard_map/while/body/eval_jaxpr/arxb,sab->rsx/dot_general | solution.py:56
  92.2 2.3 %fusion.30 = f32[2,8,512]{2,1,0:T(8,128)S(1)} fusion(f32[2,2,512]{2,0,1:T(2,128)S(1)} %get-tuple-element.183, s32[2,2,512]{2,0,1:T(2,128)S(1)} %get-tuple-element.184, f32[2,2,512]{2,0,1:T(2,128)S(1)} %get-tuple-element.185, s32[2,2,512]{2,0,1:T(2,128)S(1)} %get-tuple-element.186, f32[2,8,512]{2,1,0:T(8,128)S(1)} %get-tuple-element.196, ...), kind=kOutput, calls=%fused_computation.5.clone.1 | convolution fusion | flops 46153728 | bytes 131077 | tf_op jit(solution)/shard_map/while/body/eval_jaxpr/arxb,sab->rsx/dot_general | solution.py:56
  94.5 2.3 %fusion.30 = f32[2,8,512]{2,1,0:T(8,128)S(1)} fusion(f32[2,2,512]{2,0,1:T(2,128)S(1)} %get-tuple-element.183, s32[2,2,512]{2,0,1:T(2,128)S(1)} %get-tuple-element.184, f32[2,2,512]{2,0,1:T(2,128)S(1)} %get-tuple-element.185, s32[2,2,512]{2,0,1:T(2,128)S(1)} %get-tuple-element.186, f32[2,8,512]{2,1,0:T(8,128)S(1)} %get-tuple-element.196, ...), kind=kOutput, calls=%fused_computation.5.clone.1 | convolution fusion | flops 46153728 | bytes 131077 | tf_op jit(solution)/shard_map/while/body/eval_jaxpr/arxb,sab->rsx/dot_general | solution.py:56
  96.9 2.3 %fusion.30 = f32[2,8,512]{2,1,0:T(8,128)S(1)} fusion(f32[2,2,512]{2,0,1:T(2,128)S(1)} %get-tuple-element.183, s32[2,2,512]{2,0,1:T(2,128)S(1)} %get-tuple-element.184, f32[2,2,512]{2,0,1:T(2,128)S(1)} %get-tuple-element.185, s32[2,2,512]{2,0,1:T(2,128)S(1)} %get-tuple-element.186, f32[2,8,512]{2,1,0:T(8,128)S(1)} %get-tuple-element.196, ...), kind=kOutput, calls=%fused_computation.5.clone.1 | convolution fusion | flops 46153728 | bytes 131077 | tf_op jit(solution)/shard_map/while/body/eval_jaxpr/arxb,sab->rsx/dot_general | solution.py:56
  99.2 2.3 %fusion.30 = f32[2,8,512]{2,1,0:T(8,128)S(1)} fusion(f32[2,2,512]{2,0,1:T(2,128)S(1)} %get-tuple-element.183, s32[2,2,512]{2,0,1:T(2,128)S(1)} %get-tuple-element.184, f32[2,2,512]{2,0,1:T(2,128)S(1)} %get-tuple-element.185, s32[2,2,512]{2,0,1:T(2,128)S(1)} %get-tuple-element.186, f32[2,8,512]{2,1,0:T(8,128)S(1)} %get-tuple-element.196, ...), kind=kOutput, calls=%fused_computation.5.clone.1 | convolution fusion | flops 46153728 | bytes 131077 | tf_op jit(solution)/shard_map/while/body/eval_jaxpr/arxb,sab->rsx/dot_general | solution.py:56
  101.5 2.3 %fusion.30 = f32[2,8,512]{2,1,0:T(8,128)S(1)} fusion(f32[2,2,512]{2,0,1:T(2,128)S(1)} %get-tuple-element.183, s32[2,2,512]{2,0,1:T(2,128)S(1)} %get-tuple-element.184, f32[2,2,512]{2,0,1:T(2,128)S(1)} %get-tuple-element.185, s32[2,2,512]{2,0,1:T(2,128)S(1)} %get-tuple-element.186, f32[2,8,512]{2,1,0:T(8,128)S(1)} %get-tuple-element.196, ...), kind=kOutput, calls=%fused_computation.5.clone.1 | convolution fusion | flops 46153728 | bytes 131077 | tf_op jit(solution)/shard_map/while/body/eval_jaxpr/arxb,sab->rsx/dot_general | solution.py:56
  103.9 2.3 %fusion.30 = f32[2,8,512]{2,1,0:T(8,128)S(1)} fusion(f32[2,2,512]{2,0,1:T(2,128)S(1)} %get-tuple-element.183, s32[2,2,512]{2,0,1:T(2,128)S(1)} %get-tuple-element.184, f32[2,2,512]{2,0,1:T(2,128)S(1)} %get-tuple-element.185, s32[2,2,512]{2,0,1:T(2,128)S(1)} %get-tuple-element.186, f32[2,8,512]{2,1,0:T(8,128)S(1)} %get-tuple-element.196, ...), kind=kOutput, calls=%fused_computation.5.clone.1 | convolution fusion | flops 46153728 | bytes 131077 | tf_op jit(solution)/shard_map/while/body/eval_jaxpr/arxb,sab->rsx/dot_general | solution.py:56
  106.2 2.3 %fusion.30 = f32[2,8,512]{2,1,0:T(8,128)S(1)} fusion(f32[2,2,512]{2,0,1:T(2,128)S(1)} %get-tuple-element.183, s32[2,2,512]{2,0,1:T(2,128)S(1)} %get-tuple-element.184, f32[2,2,512]{2,0,1:T(2,128)S(1)} %get-tuple-element.185, s32[2,2,512]{2,0,1:T(2,128)S(1)} %get-tuple-element.186, f32[2,8,512]{2,1,0:T(8,128)S(1)} %get-tuple-element.196, ...), kind=kOutput, calls=%fused_computation.5.clone.1 | convolution fusion | flops 46153728 | bytes 131077 | tf_op jit(solution)/shard_map/while/body/eval_jaxpr/arxb,sab->rsx/dot_general | solution.py:56
  108.6 2.3 %fusion.30 = f32[2,8,512]{2,1,0:T(8,128)S(1)} fusion(f32[2,2,512]{2,0,1:T(2,128)S(1)} %get-tuple-element.183, s32[2,2,512]{2,0,1:T(2,128)S(1)} %get-tuple-element.184, f32[2,2,512]{2,0,1:T(2,128)S(1)} %get-tuple-element.185, s32[2,2,512]{2,0,1:T(2,128)S(1)} %get-tuple-element.186, f32[2,8,512]{2,1,0:T(8,128)S(1)} %get-tuple-element.196, ...), kind=kOutput, calls=%fused_computation.5.clone.1 | convolution fusion | flops 46153728 | bytes 131077 | tf_op jit(solution)/shard_map/while/body/eval_jaxpr/arxb,sab->rsx/dot_general | solution.py:56
  110.9 2.3 %fusion.30 = f32[2,8,512]{2,1,0:T(8,128)S(1)} fusion(f32[2,2,512]{2,0,1:T(2,128)S(1)} %get-tuple-element.183, s32[2,2,512]{2,0,1:T(2,128)S(1)} %get-tuple-element.184, f32[2,2,512]{2,0,1:T(2,128)S(1)} %get-tuple-element.185, s32[2,2,512]{2,0,1:T(2,128)S(1)} %get-tuple-element.186, f32[2,8,512]{2,1,0:T(8,128)S(1)} %get-tuple-element.196, ...), kind=kOutput, calls=%fused_computation.5.clone.1 | convolution fusion | flops 46153728 | bytes 131077 | tf_op jit(solution)/shard_map/while/body/eval_jaxpr/arxb,sab->rsx/dot_general | solution.py:56
  113.2 2.3 %fusion.30 = f32[2,8,512]{2,1,0:T(8,128)S(1)} fusion(f32[2,2,512]{2,0,1:T(2,128)S(1)} %get-tuple-element.183, s32[2,2,512]{2,0,1:T(2,128)S(1)} %get-tuple-element.184, f32[2,2,512]{2,0,1:T(2,128)S(1)} %get-tuple-element.185, s32[2,2,512]{2,0,1:T(2,128)S(1)} %get-tuple-element.186, f32[2,8,512]{2,1,0:T(8,128)S(1)} %get-tuple-element.196, ...), kind=kOutput, calls=%fused_computation.5.clone.1 | convolution fusion | flops 46153728 | bytes 131077 | tf_op jit(solution)/shard_map/while/body/eval_jaxpr/arxb,sab->rsx/dot_general | solution.py:56
  115.6 2.3 %fusion.30 = f32[2,8,512]{2,1,0:T(8,128)S(1)} fusion(f32[2,2,512]{2,0,1:T(2,128)S(1)} %get-tuple-element.183, s32[2,2,512]{2,0,1:T(2,128)S(1)} %get-tuple-element.184, f32[2,2,512]{2,0,1:T(2,128)S(1)} %get-tuple-element.185, s32[2,2,512]{2,0,1:T(2,128)S(1)} %get-tuple-element.186, f32[2,8,512]{2,1,0:T(8,128)S(1)} %get-tuple-element.196, ...), kind=kOutput, calls=%fused_computation.5.clone.1 | convolution fusion | flops 46153728 | bytes 131077 | tf_op jit(solution)/shard_map/while/body/eval_jaxpr/arxb,sab->rsx/dot_general | solution.py:56
  117.9 2.3 %fusion.30 = f32[2,8,512]{2,1,0:T(8,128)S(1)} fusion(f32[2,2,512]{2,0,1:T(2,128)S(1)} %get-tuple-element.183, s32[2,2,512]{2,0,1:T(2,128)S(1)} %get-tuple-element.184, f32[2,2,512]{2,0,1:T(2,128)S(1)} %get-tuple-element.185, s32[2,2,512]{2,0,1:T(2,128)S(1)} %get-tuple-element.186, f32[2,8,512]{2,1,0:T(8,128)S(1)} %get-tuple-element.196, ...), kind=kOutput, calls=%fused_computation.5.clone.1 | convolution fusion | flops 46153728 | bytes 131077 | tf_op jit(solution)/shard_map/while/body/eval_jaxpr/arxb,sab->rsx/dot_general | solution.py:56
  120.3 2.3 %fusion.30 = f32[2,8,512]{2,1,0:T(8,128)S(1)} fusion(f32[2,2,512]{2,0,1:T(2,128)S(1)} %get-tuple-element.183, s32[2,2,512]{2,0,1:T(2,128)S(1)} %get-tuple-element.184, f32[2,2,512]{2,0,1:T(2,128)S(1)} %get-tuple-element.185, s32[2,2,512]{2,0,1:T(2,128)S(1)} %get-tuple-element.186, f32[2,8,512]{2,1,0:T(8,128)S(1)} %get-tuple-element.196, ...), kind=kOutput, calls=%fused_computation.5.clone.1 | convolution fusion | flops 46153728 | bytes 131077 | tf_op jit(solution)/shard_map/while/body/eval_jaxpr/arxb,sab->rsx/dot_general | solution.py:56
  122.6 2.3 %fusion.30 = f32[2,8,512]{2,1,0:T(8,128)S(1)} fusion(f32[2,2,512]{2,0,1:T(2,128)S(1)} %get-tuple-element.183, s32[2,2,512]{2,0,1:T(2,128)S(1)} %get-tuple-element.184, f32[2,2,512]{2,0,1:T(2,128)S(1)} %get-tuple-element.185, s32[2,2,512]{2,0,1:T(2,128)S(1)} %get-tuple-element.186, f32[2,8,512]{2,1,0:T(8,128)S(1)} %get-tuple-element.196, ...), kind=kOutput, calls=%fused_computation.5.clone.1 | convolution fusion | flops 46153728 | bytes 131077 | tf_op jit(solution)/shard_map/while/body/eval_jaxpr/arxb,sab->rsx/dot_general | solution.py:56
  124.9 2.3 %fusion.30 = f32[2,8,512]{2,1,0:T(8,128)S(1)} fusion(f32[2,2,512]{2,0,1:T(2,128)S(1)} %get-tuple-element.183, s32[2,2,512]{2,0,1:T(2,128)S(1)} %get-tuple-element.184, f32[2,2,512]{2,0,1:T(2,128)S(1)} %get-tuple-element.185, s32[2,2,512]{2,0,1:T(2,128)S(1)} %get-tuple-element.186, f32[2,8,512]{2,1,0:T(8,128)S(1)} %get-tuple-element.196, ...), kind=kOutput, calls=%fused_computation.5.clone.1 | convolution fusion | flops 46153728 | bytes 131077 | tf_op jit(solution)/shard_map/while/body/eval_jaxpr/arxb,sab->rsx/dot_general | solution.py:56
  127.3 2.3 %fusion.30 = f32[2,8,512]{2,1,0:T(8,128)S(1)} fusion(f32[2,2,512]{2,0,1:T(2,128)S(1)} %get-tuple-element.183, s32[2,2,512]{2,0,1:T(2,128)S(1)} %get-tuple-element.184, f32[2,2,512]{2,0,1:T(2,128)S(1)} %get-tuple-element.185, s32[2,2,512]{2,0,1:T(2,128)S(1)} %get-tuple-element.186, f32[2,8,512]{2,1,0:T(8,128)S(1)} %get-tuple-element.196, ...), kind=kOutput, calls=%fused_computation.5.clone.1 | convolution fusion | flops 46153728 | bytes 131077 | tf_op jit(solution)/shard_map/while/body/eval_jaxpr/arxb,sab->rsx/dot_general | solution.py:56
  129.6 2.3 %fusion.30 = f32[2,8,512]{2,1,0:T(8,128)S(1)} fusion(f32[2,2,512]{2,0,1:T(2,128)S(1)} %get-tuple-element.183, s32[2,2,512]{2,0,1:T(2,128)S(1)} %get-tuple-element.184, f32[2,2,512]{2,0,1:T(2,128)S(1)} %get-tuple-element.185, s32[2,2,512]{2,0,1:T(2,128)S(1)} %get-tuple-element.186, f32[2,8,512]{2,1,0:T(8,128)S(1)} %get-tuple-element.196, ...), kind=kOutput, calls=%fused_computation.5.clone.1 | convolution fusion | flops 46153728 | bytes 131077 | tf_op jit(solution)/shard_map/while/body/eval_jaxpr/arxb,sab->rsx/dot_general | solution.py:56
  132.0 2.3 %fusion.30 = f32[2,8,512]{2,1,0:T(8,128)S(1)} fusion(f32[2,2,512]{2,0,1:T(2,128)S(1)} %get-tuple-element.183, s32[2,2,512]{2,0,1:T(2,128)S(1)} %get-tuple-element.184, f32[2,2,512]{2,0,1:T(2,128)S(1)} %get-tuple-element.185, s32[2,2,512]{2,0,1:T(2,128)S(1)} %get-tuple-element.186, f32[2,8,512]{2,1,0:T(8,128)S(1)} %get-tuple-element.196, ...), kind=kOutput, calls=%fused_computation.5.clone.1 | convolution fusion | flops 46153728 | bytes 131077 | tf_op jit(solution)/shard_map/while/body/eval_jaxpr/arxb,sab->rsx/dot_general | solution.py:56
  134.3 2.3 %fusion.30 = f32[2,8,512]{2,1,0:T(8,128)S(1)} fusion(f32[2,2,512]{2,0,1:T(2,128)S(1)} %get-tuple-element.183, s32[2,2,512]{2,0,1:T(2,128)S(1)} %get-tuple-element.184, f32[2,2,512]{2,0,1:T(2,128)S(1)} %get-tuple-element.185, s32[2,2,512]{2,0,1:T(2,128)S(1)} %get-tuple-element.186, f32[2,8,512]{2,1,0:T(8,128)S(1)} %get-tuple-element.196, ...), kind=kOutput, calls=%fused_computation.5.clone.1 | convolution fusion | flops 46153728 | bytes 131077 | tf_op jit(solution)/shard_map/while/body/eval_jaxpr/arxb,sab->rsx/dot_general | solution.py:56
  136.6 2.3 %fusion.30 = f32[2,8,512]{2,1,0:T(8,128)S(1)} fusion(f32[2,2,512]{2,0,1:T(2,128)S(1)} %get-tuple-element.183, s32[2,2,512]{2,0,1:T(2,128)S(1)} %get-tuple-element.184, f32[2,2,512]{2,0,1:T(2,128)S(1)} %get-tuple-element.185, s32[2,2,512]{2,0,1:T(2,128)S(1)} %get-tuple-element.186, f32[2,8,512]{2,1,0:T(8,128)S(1)} %get-tuple-element.196, ...), kind=kOutput, calls=%fused_computation.5.clone.1 | convolution fusion | flops 46153728 | bytes 131077 | tf_op jit(solution)/shard_map/while/body/eval_jaxpr/arxb,sab->rsx/dot_general | solution.py:56
  139.0 2.3 %fusion.30 = f32[2,8,512]{2,1,0:T(8,128)S(1)} fusion(f32[2,2,512]{2,0,1:T(2,128)S(1)} %get-tuple-element.183, s32[2,2,512]{2,0,1:T(2,128)S(1)} %get-tuple-element.184, f32[2,2,512]{2,0,1:T(2,128)S(1)} %get-tuple-element.185, s32[2,2,512]{2,0,1:T(2,128)S(1)} %get-tuple-element.186, f32[2,8,512]{2,1,0:T(8,128)S(1)} %get-tuple-element.196, ...), kind=kOutput, calls=%fused_computation.5.clone.1 | convolution fusion | flops 46153728 | bytes 131077 | tf_op jit(solution)/shard_map/while/body/eval_jaxpr/arxb,sab->rsx/dot_general | solution.py:56
  141.3 2.3 %fusion.30 = f32[2,8,512]{2,1,0:T(8,128)S(1)} fusion(f32[2,2,512]{2,0,1:T(2,128)S(1)} %get-tuple-element.183, s32[2,2,512]{2,0,1:T(2,128)S(1)} %get-tuple-element.184, f32[2,2,512]{2,0,1:T(2,128)S(1)} %get-tuple-element.185, s32[2,2,512]{2,0,1:T(2,128)S(1)} %get-tuple-element.186, f32[2,8,512]{2,1,0:T(8,128)S(1)} %get-tuple-element.196, ...), kind=kOutput, calls=%fused_computation.5.clone.1 | convolution fusion | flops 46153728 | bytes 131077 | tf_op jit(solution)/shard_map/while/body/eval_jaxpr/arxb,sab->rsx/dot_general | solution.py:56
  143.7 2.3 %fusion.30 = f32[2,8,512]{2,1,0:T(8,128)S(1)} fusion(f32[2,2,512]{2,0,1:T(2,128)S(1)} %get-tuple-element.183, s32[2,2,512]{2,0,1:T(2,128)S(1)} %get-tuple-element.184, f32[2,2,512]{2,0,1:T(2,128)S(1)} %get-tuple-element.185, s32[2,2,512]{2,0,1:T(2,128)S(1)} %get-tuple-element.186, f32[2,8,512]{2,1,0:T(8,128)S(1)} %get-tuple-element.196, ...), kind=kOutput, calls=%fused_computation.5.clone.1 | convolution fusion | flops 46153728 | bytes 131077 | tf_op jit(solution)/shard_map/while/body/eval_jaxpr/arxb,sab->rsx/dot_general | solution.py:56
  146.0 2.3 %fusion.30 = f32[2,8,512]{2,1,0:T(8,128)S(1)} fusion(f32[2,2,512]{2,0,1:T(2,128)S(1)} %get-tuple-element.183, s32[2,2,512]{2,0,1:T(2,128)S(1)} %get-tuple-element.184, f32[2,2,512]{2,0,1:T(2,128)S(1)} %get-tuple-element.185, s32[2,2,512]{2,0,1:T(2,128)S(1)} %get-tuple-element.186, f32[2,8,512]{2,1,0:T(8,128)S(1)} %get-tuple-element.196, ...), kind=kOutput, calls=%fused_computation.5.clone.1 | convolution fusion | flops 46153728 | bytes 131077 | tf_op jit(solution)/shard_map/while/body/eval_jaxpr/arxb,sab->rsx/dot_general | solution.py:56
  148.3 2.3 %fusion.30 = f32[2,8,512]{2,1,0:T(8,128)S(1)} fusion(f32[2,2,512]{2,0,1:T(2,128)S(1)} %get-tuple-element.183, s32[2,2,512]{2,0,1:T(2,128)S(1)} %get-tuple-element.184, f32[2,2,512]{2,0,1:T(2,128)S(1)} %get-tuple-element.185, s32[2,2,512]{2,0,1:T(2,128)S(1)} %get-tuple-element.186, f32[2,8,512]{2,1,0:T(8,128)S(1)} %get-tuple-element.196, ...), kind=kOutput, calls=%fused_computation.5.clone.1 | convolution fusion | flops 46153728 | bytes 131077 | tf_op jit(solution)/shard_map/while/body/eval_jaxpr/arxb,sab->rsx/dot_general | solution.py:56
  150.7 2.3 %fusion.30 = f32[2,8,512]{2,1,0:T(8,128)S(1)} fusion(f32[2,2,512]{2,0,1:T(2,128)S(1)} %get-tuple-element.183, s32[2,2,512]{2,0,1:T(2,128)S(1)} %get-tuple-element.184, f32[2,2,512]{2,0,1:T(2,128)S(1)} %get-tuple-element.185, s32[2,2,512]{2,0,1:T(2,128)S(1)} %get-tuple-element.186, f32[2,8,512]{2,1,0:T(8,128)S(1)} %get-tuple-element.196, ...), kind=kOutput, calls=%fused_computation.5.clone.1 | convolution fusion | flops 46153728 | bytes 131077 | tf_op jit(solution)/shard_map/while/body/eval_jaxpr/arxb,sab->rsx/dot_general | solution.py:56
  152.9 0.6 broadcast_multiply_fusion
  (100 shorter events, 1.9 us)
Async XLA Ops:
  1.5 21.5 %all-to-all-start.1 = ((s32[8,2,8,512]{3,2,1,0:T(8,128)}), s32[8,2,8,512]{3,2,1,0:T(8,128)S(1)}, u32[]{:S(2)}, u32[]{:S(2)}) async-start(s32[8,2,8,512]{3,2,1,0:T(8,128)} %broadcast_in_dim.84), calls=%async_computation.1 | async-start | bytes 524288 | tf_op jit(solution)/shard_map/all_to_all | solution.py:11
  23.9 21.6 %all-to-all-start.2 = ((s32[2,64,512]{2,0,1:T(2,128)}), s32[2,64,512]{2,0,1:T(2,128)S(1)}, u32[]{:S(2)}, u32[]{:S(2)}) async-start(s32[2,64,512]{2,0,1:T(2,128)} %copy.12), calls=%async_computation.2 | async-start | bytes 524288 | tf_op jit(solution)/shard_map/all_to_all | solution.py:70
  46.6 31.4 %all-to-all-start = ((bf16[32,8,2,1024]{3,1,2,0:T(8,128)(2,1)}), bf16[32,8,2,1024]{3,1,2,0:T(8,128)(2,1)S(1)}, u32[]{:S(2)}, u32[]{:S(2)}) async-start(bf16[32,8,2,1024]{3,1,2,0:T(8,128)(2,1)} %broadcast_in_dim.83), calls=%async_computation | async-start | bytes 2097152 | tf_op jit(solution)/shard_map/all_to_all | solution.py:11
where the time goes:
time: 154 us
  matrix products  75.6 us (49%)
  waiting for transfers between devices  44.9 us (29%)
  starting transfers between devices  25.5 us (17%)
  local copies, waits for them, and re-layouts  4.48 us (3%)
  other arithmetic  2.41 us (2%)
    dot_general x32, matrix products, project_block(): jnp.einsum('arxb,sab->rsx', weights, projections, preferred_element_type=...  72.4 us
    all_to_all x2, waiting for transfers between devices, sent_to_all(): lax.all_to_all(jnp.broadcast_to(array[None], (devices, *array.shape)), ax...  36.9 us
    all_to_all x2, starting transfers between devices, sent_to_all(): lax.all_to_all(jnp.broadcast_to(array[None], (devices, *array.shape)), ax...  15.2 us
    all_to_all x1, starting transfers between devices, shards(): lax.all_to_all(coord_table, 'ang', split_axis=1, concat_axis=0, tiled=True)  10.3 us
    all_to_all x1, waiting for transfers between devices, shards(): lax.all_to_all(coord_table, 'ang', split_axis=1, concat_axis=0, tiled=True)  8.01 us
    dot_general x1, matrix products, shards(): jnp.dot(sinogram.reshape(slices * angles, bin_count), table, preferred_el...  3.19 us
  transfers between devices with their start and end apart: 3, of which 3 were waited for; matrix products, arithmetic and copies ran while one was open for 3% of the time, Pallas kernels for 0%

commit v1 on v0

v1 whole, which is shorter than its diff:
```python
import math

import jax
import jax.numpy as jnp
from jax import lax
from jax.experimental import pallas as pl
from jax.experimental.pallas import tpu as pltpu
from jax.sharding import PartitionSpec as P

MESH = pl.DeviceIdType.MESH
NY, NZ, NC, NH, NX = 4, 4, 2, 2, 4
NK = NY * NC


def flip(bit, by):
    return bit + by - 2 * bit * by


def lane_gather(table, lanes):
    return jnp.take_along_axis(table, lanes, axis=1, mode="promise_in_bounds")


def write_ramp(g_ref):
    depth, width = g_ref.shape

    def chunk(step, carry):
        base = pl.multiple_of(step * 16, 16)
        for lane in range(0, width, 256):
            row = lax.broadcasted_iota(jnp.int32, (16, 256), 0) + base
            column = lax.broadcasted_iota(jnp.int32, (16, 256), 1) + (lane - 768)
            offset = column - row
            real = offset.astype(jnp.float32)
            square = jnp.maximum(real * real, jnp.float32(1.0))
            odd = (offset & 1) != 0
            value = jnp.where(odd, jnp.float32(-1.0 / math.pi**2) / square, jnp.float32(0.0))
            value = jnp.where(offset == 0, jnp.float32(0.25), value)
            g_ref[pl.ds(base, 16), lane : lane + 256] = value.astype(jnp.bfloat16)
        return carry

    lax.fori_loop(0, depth // 16, chunk, 0)


def kernel(
    x_ref, c_ref, o_ref,
    csend, sbuf, cbuf, g_ref, f_ref, t_ref, sc_ref, obuf, rbuf,
    s_send, s_recv, c_send, c_recv, w_send, w_recv, o_send, o_recv,
):
    ang, sl = lax.axis_index("ang"), lax.axis_index("sl")
    y, z, c = ang // 8, (ang // 2) % 4, ang % 2
    h, x = sl // 4, sl % 4

    def device(yy, zz, cc, hh, xx):
        return (yy * 8 + zz * 2 + cc, hh * 4 + xx)

    def near(dy, dc, dh):
        return device((y + dy) % NY, z, flip(c, dc), flip(h, dh), x)

    along_x = [device(y, z, c, h, (x + dx) % NX) for dx in range(1, NX)]
    owners = []
    for dh in range(NH):
        for dx in range(NX):
            block = flip(h, dh) * NX + (x - dx) % NX
            owners.append((4 * block + y, sl))
    sources = [((ang % 4) * 8 + zz * 2 + cc, sl) for zz in range(NZ) for cc in range(NC)]

    barrier = pltpu.get_barrier_semaphore()
    group = [near(dy, dc, dh) for dh in range(NH) for dy in range(NY) for dc in range(NC)][1:]
    group += along_x + owners + sources
    for other in group:
        pl.semaphore_signal(barrier, inc=1, device_id=other, device_id_type=MESH)
    for a in range(2):
        for p in range(4):
            csend[:, a, p, :] = c_ref[a, :, 128 * p : 128 * (p + 1)]
    pl.semaphore_wait(barrier, len(group))

    first = {}
    for dh in (1, 0):
        for dy in range(NY):
            for dc in range(NC):
                k = dy * NC + dc
                row = 2 * ((y + dy) % NY) + flip(c, dc)
                if (dh, k) == (0, 0):
                    cbuf[0, :, 0, :, :] = csend[row]
                    continue
                copy = pltpu.make_async_remote_copy(
                    src_ref=csend.at[row],
                    dst_ref=cbuf.at[k, :, dh * NX],
                    send_sem=c_send.at[dh, k],
                    recv_sem=c_recv.at[dh, k],
                    device_id=near(dy, dc, dh),
                    device_id_type=MESH,
                )
                copy.start()
                first[dh, k] = copy
    sino = []
    for dy in range(NY):
        for dc in range(NC):
            k = dy * NC + dc
            if k == 0:
                sbuf[0] = x_ref[...]
                continue
            copy = pltpu.make_async_remote_copy(
                src_ref=x_ref,
                dst_ref=sbuf.at[k],
                send_sem=s_send.at[k],
                recv_sem=s_recv.at[k],
                device_id=near(dy, dc, 0),
                device_id_type=MESH,
            )
            copy.start()
            sino.append(copy)

    write_ramp(g_ref)

    def forward(dh):
        copies = []
        for k in range(NK):
            if (dh, k) in first:
                first[dh, k].wait_recv()
        for dx in range(1, NX):
            copy = pltpu.make_async_remote_copy(
                src_ref=cbuf.at[:, :, dh * NX],
                dst_ref=cbuf.at[:, :, dh * NX + dx],
                send_sem=w_send.at[dh, dx],
                recv_sem=w_recv.at[dh, dx],
                device_id=along_x[dx - 1],
                device_id_type=MESH,
            )
            copy.start()
            copies.append(copy)
        return copies

    passed = {0: forward(0), 1: forward(1)}

    for copy in sino:
        copy.wait_recv()
    lhs = sbuf[...].reshape(NK * 16, 1024)
    for n in range(4):
        total = None
        for m in range(4):
            at = 768 - 256 * m + 256 * n
            part = jnp.dot(
                lhs[:, 256 * m : 256 * (m + 1)], g_ref[:, at : at + 256],
                preferred_element_type=jnp.float32,
            )
            total = part if total is None else total + part
        f_ref[2 * n] = total[:, :128]
        f_ref[2 * n + 1] = total[:, 128:]

    def pack(k, carry):
        for a in range(2):
            rows = pl.ds(k * 16 + a, 8, stride=2)
            value = jnp.concatenate([f_ref[n, rows, :] for n in range(8)], axis=1)
            top = jnp.maximum(jnp.max(jnp.abs(value), axis=1, keepdims=True), jnp.float32(1e-30))
            fixed = (value * (jnp.float32(32767.0) / top) + jnp.float32(32768.5)).astype(jnp.int32)
            fixed = fixed - 32768
            after = pltpu.roll(fixed, 1023, 1)
            t_ref[k, a] = (fixed << 16) | (after & 0xFFFF)
            sc_ref[k, a] = jnp.broadcast_to(top * jnp.float32(1.0 / 32767.0), (8, 128))
        return carry

    lax.fori_loop(0, NK, pack, 0)

    own = z * NC + c
    sent = []
    for dh in range(NH):
        for copy in passed[dh]:
            copy.wait_recv()

        def source(k, sums, dh=dh):
            sums = list(sums)
            for a in range(2):
                table = [t_ref[k, a, :, 128 * n : 128 * (n + 1)] for n in range(8)]
                scale = sc_ref[k, a]
                for dx in range(NX):
                    for p in range(4):
                        coord = cbuf[k, a, dh * NX + dx, p : p + 1, :]
                        coord = jnp.broadcast_to(coord, (8, 128))
                        left = coord >> 20
                        fraction = (coord & 0xFFFFF).astype(jnp.float32)
                        fraction = fraction * jnp.float32(1.0 / 1048576.0)
                        lanes = left & 127
                        found = [lane_gather(part, lanes) for part in table]
                        for bit in (128, 256, 512):
                            on = (left & bit) != 0
                            found = [
                                jnp.where(on, found[i + 1], found[i])
                                for i in range(0, len(found), 2)
                            ]
                        word = found[0]
                        low = (word >> 16).astype(jnp.float32)
                        high = ((word << 16) >> 16).astype(jnp.float32)
                        value = low + (high - low) * fraction
                        at = dx * 4 + p
                        sums[at] = sums[at] + value * scale
            return tuple(sums)

        zero = jnp.zeros((8, 128), jnp.float32)
        sums = lax.fori_loop(0, NK, source, (zero,) * 16)
        for dx in range(NX):
            slot = dh * NX + dx
            for p in range(4):
                obuf[slot, :, 128 * p : 128 * (p + 1)] = sums[dx * 4 + p].astype(jnp.bfloat16)
            copy = pltpu.make_async_remote_copy(
                src_ref=obuf.at[slot],
                dst_ref=rbuf.at[own],
                send_sem=o_send.at[slot],
                recv_sem=o_recv.at[own],
                device_id=owners[slot],
                device_id_type=MESH,
            )
            mine = owners[slot][0] == ang

            @pl.when(jnp.logical_not(mine))
            def _():
                copy.start()

            @pl.when(mine)
            def _():
                rbuf[own] = obuf[slot]

            sent.append((copy, mine))

    for at, source_device in enumerate(sources):
        arrival = pltpu.make_async_remote_copy(
            src_ref=obuf.at[0],
            dst_ref=rbuf.at[at],
            send_sem=o_send.at[0],
            recv_sem=o_recv.at[at],
            device_id=source_device,
            device_id_type=MESH,
        )

        @pl.when(source_device[0] != ang)
        def _():
            arrival.wait_recv()

    for cc in range(NC):
        total = rbuf[cc].astype(jnp.float32)
        for zz in range(1, NZ):
            total = total + rbuf[zz * NC + cc].astype(jnp.float32)
        o_ref[cc] = total * jnp.float32(math.pi / 64)

    for copy, mine in sent:

        @pl.when(jnp.logical_not(mine))
        def _():
            copy.wait_send()

    for copy in [*first.values(), *sino, *passed[0], *passed[1]]:
        copy.wait_send()


def shards(sinogram, detector_coord):
    dma = pltpu.SemaphoreType.DMA
    vmem = pl.BlockSpec(memory_space=pltpu.VMEM)
    return pl.pallas_call(
        kernel,
        out_shape=jax.ShapeDtypeStruct((2, 8, 512), jnp.float32),
        in_specs=[vmem, vmem],
        out_specs=vmem,
        scratch_shapes=[
            pltpu.VMEM((8, 2, 4, 128), jnp.int32),
            pltpu.VMEM((NK, 8, 2, 1024), jnp.bfloat16),
            pltpu.VMEM((NK, 2, 8, 4, 128), jnp.int32),
            pltpu.VMEM((256, 1792), jnp.bfloat16),
            pltpu.VMEM((8, NK * 16, 128), jnp.float32),
            pltpu.VMEM((NK, 2, 8, 1024), jnp.int32),
            pltpu.VMEM((NK, 2, 8, 128), jnp.float32),
            pltpu.VMEM((8, 8, 512), jnp.bfloat16),
            pltpu.VMEM((8, 8, 512), jnp.bfloat16),
            dma((NK,)), dma((NK,)),
            dma((NH, NK)), dma((NH, NK)),
            dma((NH, NX)), dma((NH, NX)),
            dma((8,)), dma((8,)),
        ],
        compiler_params=pltpu.CompilerParams(collective_id=0, has_side_effects=True),
    )(sinogram, detector_coord)


def solution(mesh):
    in_specs = (P("sl", "ang", None), P("ang", "sl", None))
    out_specs = P("ang", "sl", None)
    return jax.shard_map(shards, mesh=mesh, in_specs=in_specs, out_specs=out_specs, check_vma=False)
```

time: 154 us -> 33.2 us (0.22)
  the two profiles are of different devices: /device:TPU:1 before, /device:TPU:25 now
where the time goes in v1:
time: 33.2 us; the launch traced here: 32.7 us
  Pallas kernels  31.3 us (94%)
  local copies, waits for them, and re-layouts  1.38 us (4%)
    pallas_call x1, Pallas kernels, shards(): pl.pallas_call(kernel, out_shape=jax.ShapeDtypeStruct((2, 8, 512), jnp.fl...  31.3 us
    unnamed x1, local copies, waits for them, and re-layouts  1.38 us

profile of v1, /device:TPU:25, one launch (start us, length us, event | category | flops | bytes accessed | tf_op | source)
XLA Modules:
  0.0 32.7 jit_solution(8307902612021958044)
XLA Ops:
  0.0 31.3 %shard_map.28 = f32[2,8,512]{2,1,0:T(8,128)} custom-call(bf16[8,2,1024]{2,1,0:T(2,128)(2,1)} %x_ref.1, s32[2,8,512]{2,1,0:T(8,128)} %c_ref.1), custom_call_target="tpu_custom_call" | custom-call | tf_op jit(solution)/shard_map/pallas_call | solution.py:257
  31.3 1.4 %copy.4 = f32[2,8,512]{2,1,0:T(8,128)} copy(f32[2,8,512]{2,1,0:T(8,128)} %shard_map.28) | data formatting | bytes 65536

commit v2 on v1

--- a/solution.py
+++ b/solution.py
@@ -42,8 +42,8 @@
 
 def kernel(
     x_ref, c_ref, o_ref,
-    csend, sbuf, cbuf, g_ref, f_ref, t_ref, sc_ref, obuf, rbuf,
-    s_send, s_recv, c_send, c_recv, w_send, w_recv, o_send, o_recv,
+    csend, hbuf, sbuf, cbuf, g_ref, f_ref, t_ref, sc_ref, obuf, rbuf,
+    s_send, s_recv, h_send, h_recv, c_send, c_recv, o_send, o_recv,
 ):
     ang, sl = lax.axis_index("ang"), lax.axis_index("sl")
     y, z, c = ang // 8, (ang // 2) % 4, ang % 2
@@ -52,10 +52,11 @@
     def device(yy, zz, cc, hh, xx):
         return (yy * 8 + zz * 2 + cc, hh * 4 + xx)
 
-    def near(dy, dc, dh):
-        return device((y + dy) % NY, z, flip(c, dc), flip(h, dh), x)
-
-    along_x = [device(y, z, c, h, (x + dx) % NX) for dx in range(1, NX)]
+    def near(dy, dc, dx):
+        return device((y + dy) % NY, z, flip(c, dc), h, (x + dx) % NX)
+
+    plane = [(dy, dc, dx) for dx in range(NX) for dy in range(NY) for dc in range(NC)][1:]
+    across = device(y, z, c, flip(h, 1), x)
     owners = []
     for dh in range(NH):
         for dx in range(NX):
@@ -64,8 +65,8 @@
     sources = [((ang % 4) * 8 + zz * 2 + cc, sl) for zz in range(NZ) for cc in range(NC)]
 
     barrier = pltpu.get_barrier_semaphore()
-    group = [near(dy, dc, dh) for dh in range(NH) for dy in range(NY) for dc in range(NC)][1:]
-    group += along_x + owners + sources
+    group = [near(*step) for step in plane] + [across]
+    group += [device(y, (z + dz) % NZ, flip(c, dc), h, x) for dz in range(1, NZ) for dc in range(NC)]
     for other in group:
         pl.semaphore_signal(barrier, inc=1, device_id=other, device_id_type=MESH)
     for a in range(2):
@@ -73,25 +74,31 @@
             csend[:, a, p, :] = c_ref[a, :, 128 * p : 128 * (p + 1)]
     pl.semaphore_wait(barrier, len(group))
 
-    first = {}
-    for dh in (1, 0):
-        for dy in range(NY):
-            for dc in range(NC):
-                k = dy * NC + dc
-                row = 2 * ((y + dy) % NY) + flip(c, dc)
-                if (dh, k) == (0, 0):
-                    cbuf[0, :, 0, :, :] = csend[row]
-                    continue
-                copy = pltpu.make_async_remote_copy(
-                    src_ref=csend.at[row],
-                    dst_ref=cbuf.at[k, :, dh * NX],
-                    send_sem=c_send.at[dh, k],
-                    recv_sem=c_recv.at[dh, k],
-                    device_id=near(dy, dc, dh),
-                    device_id_type=MESH,
-                )
-                copy.start()
-                first[dh, k] = copy
+    over = pltpu.make_async_remote_copy(
+        src_ref=csend, dst_ref=hbuf, send_sem=h_send, recv_sem=h_recv,
+        device_id=across, device_id_type=MESH,
+    )
+    over.start()
+
+    def spread(block, dh):
+        copies = []
+        for dy, dc, dx in plane:
+            k = dy * NC + dc
+            row = 2 * ((y + dy) % NY) + flip(c, dc)
+            copy = pltpu.make_async_remote_copy(
+                src_ref=block.at[row],
+                dst_ref=cbuf.at[k, :, dh * NX + dx],
+                send_sem=c_send.at[dh, k, dx],
+                recv_sem=c_recv.at[dh, k, dx],
+                device_id=near(dy, dc, dx),
+                device_id_type=MESH,
+            )
+            copy.start()
+            copies.append(copy)
+        cbuf[0, :, dh * NX, :, :] = block[2 * y + c]
+        return copies
+
+    passed = {0: spread(csend, 0)}
     sino = []
     for dy in range(NY):
         for dc in range(NC):
@@ -112,25 +119,8 @@
 
     write_ramp(g_ref)
 
-    def forward(dh):
-        copies = []
-        for k in range(NK):
-            if (dh, k) in first:
-                first[dh, k].wait_recv()
-        for dx in range(1, NX):
-            copy = pltpu.make_async_remote_copy(
-                src_ref=cbuf.at[:, :, dh * NX],
-                dst_ref=cbuf.at[:, :, dh * NX + dx],
-                send_sem=w_send.at[dh, dx],
-                recv_sem=w_recv.at[dh, dx],
-                device_id=along_x[dx - 1],
-                device_id_type=MESH,
-            )
-            copy.start()
-            copies.append(copy)
-        return copies
-
-    passed = {0: forward(0), 1: forward(1)}
+    over.wait_recv()
+    passed[1] = spread(hbuf, 1)
 
     for copy in sino:
         copy.wait_recv()
@@ -247,7 +237,7 @@
         def _():
             copy.wait_send()
 
-    for copy in [*first.values(), *sino, *passed[0], *passed[1]]:
+    for copy in [over, *sino, *passed[0], *passed[1]]:
         copy.wait_send()
 
 
@@ -261,6 +251,7 @@
         out_specs=vmem,
         scratch_shapes=[
             pltpu.VMEM((8, 2, 4, 128), jnp.int32),
+            pltpu.VMEM((8, 2, 4, 128), jnp.int32),
             pltpu.VMEM((NK, 8, 2, 1024), jnp.bfloat16),
             pltpu.VMEM((NK, 2, 8, 4, 128), jnp.int32),
             pltpu.VMEM((256, 1792), jnp.bfloat16),
@@ -270,8 +261,8 @@
             pltpu.VMEM((8, 8, 512), jnp.bfloat16),
             pltpu.VMEM((8, 8, 512), jnp.bfloat16),
             dma((NK,)), dma((NK,)),
-            dma((NH, NK)), dma((NH, NK)),
-            dma((NH, NX)), dma((NH, NX)),
+            dma(()), dma(()),
+            dma((NH, NK, NX)), dma((NH, NK, NX)),
             dma((8,)), dma((8,)),
         ],
         compiler_params=pltpu.CompilerParams(collective_id=0, has_side_effects=True),

time: 33.2 us -> 32.6 us (0.982)
  Pallas kernels: 31.3 us -> 30.8 us
    pallas_call x1, Pallas kernels: 31.3 us -> 30.8 us  [shards(): pl.pallas_call(kernel, out_shape=jax.ShapeDtypeStruct((2, 8, 512), jnp.fl...]
where the time goes in v2:
time: 32.6 us; the launch traced here: 32.1 us
  Pallas kernels  30.8 us (94%)
  local copies, waits for them, and re-layouts  1.38 us (4%)
    pallas_call x1, Pallas kernels, shards(): pl.pallas_call(kernel, out_shape=jax.ShapeDtypeStruct((2, 8, 512), jnp.fl...  30.8 us
    unnamed x1, local copies, waits for them, and re-layouts  1.38 us

profile of v2, /device:TPU:25, one launch (start us, length us, event | category | flops | bytes accessed | tf_op | source)
XLA Modules:
  0.0 32.1 jit_solution(13883357627765544299)
XLA Ops:
  0.0 30.8 %shard_map.28 = f32[2,8,512]{2,1,0:T(8,128)} custom-call(bf16[8,2,1024]{2,1,0:T(2,128)(2,1)} %x_ref.1, s32[2,8,512]{2,1,0:T(8,128)} %c_ref.1), custom_call_target="tpu_custom_call" | custom-call | tf_op jit(solution)/shard_map/pallas_call | solution.py:247
  30.8 1.4 %copy.4 = f32[2,8,512]{2,1,0:T(8,128)} copy(f32[2,8,512]{2,1,0:T(8,128)} %shard_map.28) | data formatting | bytes 65536

commit v3 on v0

v3 whole, which is shorter than its diff:
```python
import math

import jax
import jax.numpy as jnp
from jax import lax
from jax.experimental import pallas as pl
from jax.experimental.pallas import tpu as pltpu
from jax.sharding import PartitionSpec as P

MESH = pl.DeviceIdType.MESH
NY, NZ, NC, NH, NX = 4, 4, 2, 2, 4
NK = NY * NC
NB, STEP = 9, 127


def flip(bit, by):
    return bit + by - 2 * bit * by


def write_ramp(g_ref):
    depth, width = g_ref.shape

    def chunk(step, carry):
        base = pl.multiple_of(step * 16, 16)
        for lane in range(0, width, 256):
            row = lax.broadcasted_iota(jnp.int32, (16, 256), 0) + base
            column = lax.broadcasted_iota(jnp.int32, (16, 256), 1) + (lane - 768)
            offset = column - row
            real = offset.astype(jnp.float32)
            square = jnp.maximum(real * real, jnp.float32(1.0))
            odd = (offset & 1) != 0
            value = jnp.where(odd, jnp.float32(-1.0 / math.pi**2) / square, jnp.float32(0.0))
            value = jnp.where(offset == 0, jnp.float32(0.25), value)
            g_ref[pl.ds(base, 16), lane : lane + 256] = value.astype(jnp.bfloat16)
        return carry

    lax.fori_loop(0, depth // 16, chunk, 0)


def interpolate(block_values, coord, bins):
    left = coord >> 20
    fraction = (coord & 0xFFFFF).astype(jnp.float32) * jnp.float32(1.0 / 1048576.0)
    block = (left * 8257) >> 20
    within = (left - block * STEP).astype(jnp.float32)

    def rows(value):
        pair = jnp.concatenate([value, value], axis=0).astype(jnp.bfloat16)
        return jnp.concatenate([pair] * 8, axis=0)

    right = jnp.where(bins == rows(within + 1.0), rows(fraction), jnp.zeros((), jnp.bfloat16))
    weights = jnp.where(bins == rows(within), rows(1.0 - fraction), right)
    product = jnp.dot(block_values, weights, preferred_element_type=jnp.float32)
    low, high = product[0:8], product[8:16]
    for n in range(1, NB):
        here = block == n
        low = jnp.where(here, product[16 * n : 16 * n + 8], low)
        high = jnp.where(here, product[16 * n + 8 : 16 * n + 16], high)
    return low, high


def kernel(
    x_ref, c_ref, o_ref,
    csend, hbuf, sbuf, cbuf, g_ref, f_ref, v_ref, obuf,
    s_send, s_recv, h_send, h_recv, c_send, c_recv, o_send, o_recv, own_sem, tokens,
):
    ang, sl = lax.axis_index("ang"), lax.axis_index("sl")
    y, z, c = ang // 8, (ang // 2) % 4, ang % 2
    h, x = sl // 4, sl % 4
    x_high, x_low = x // 2, x % 2

    def device(yy, zz, cc, hh, xx):
        return (yy * 8 + zz * 2 + cc, hh * 4 + xx)

    def x_at(flip_high, flip_low):
        return flip(x_high, flip_high) * 2 + flip(x_low, flip_low)

    def near(dy, dc, high, low):
        return device((y + dy) % NY, z, flip(c, dc), h, x_at(high, low))

    across = device(y, z, c, flip(h, 1), x)
    twin, far_twin, sibling = near(0, 0, 0, 1), near(0, 0, 1, 0), near(0, 1, 0, 0)
    ring_y = [near(dy, 0, 0, 0) for dy in range(1, NY)]
    owners = []
    for dh in range(NH):
        for high in range(2):
            block = flip(h, dh) * NX + x_at(high, 0)
            for low in range(2):
                owners.append((4 * block + y, h * 4 + x_at(0, low)))
    row_x_low = (ang // 4) % 2
    source_sl = h * 4 + 2 * x_high + row_x_low
    sources = [((ang % 4) * 8 + zz * 2 + cc, source_sl) for zz in range(NZ) for cc in range(NC)]

    barrier = pltpu.get_barrier_semaphore()
    group = [across, twin, far_twin, *ring_y, sibling]
    group += [device(y, (z + dz) % NZ, c, h, x) for dz in range(1, NZ)]
    for other in group:
        pl.semaphore_signal(barrier, inc=1, device_id=other, device_id_type=MESH)
    for a in range(2):
        for p in range(4):
            csend[:, a, p, :] = c_ref[a, :, 128 * p : 128 * (p + 1)]
    sbuf[0] = x_ref[...]
    pl.semaphore_wait(barrier, len(group))

    over = pltpu.make_async_remote_copy(
        src_ref=csend, dst_ref=hbuf, send_sem=h_send, recv_sem=h_recv,
        device_id=across, device_id_type=MESH,
    )
    over.start()

    sino = {}

    def share(source, dy, dc, low, other):
        k = (dy * NC + dc) * 2 + low
        copy = pltpu.make_async_remote_copy(
            src_ref=source,
            dst_ref=sbuf.at[k],
            send_sem=s_send.at[k],
            recv_sem=s_recv.at[k],
            device_id=other,
            device_id_type=MESH,
        )
        copy.start()
        sino[k] = copy

    for dy in range(1, NY):
        share(x_ref, dy, 0, 0, ring_y[dy - 1])
    share(x_ref, 0, 0, 1, twin)
    share(x_ref, 0, 1, 0, sibling)
    for other in (twin, far_twin):
        pl.semaphore_signal(tokens.at[0], inc=1, device_id=other, device_id_type=MESH)
    write_ramp(g_ref)
    pl.semaphore_wait(tokens.at[0], 2)
    pl.semaphore_signal(tokens.at[1], inc=1, device_id=sibling, device_id_type=MESH)
    for dy in range(1, NY):
        share(x_ref, dy, 0, 1, near(dy, 0, 0, 1))
    pl.semaphore_wait(tokens.at[1], 1)

    def spread(block, dh):
        copies = []
        for high in range(2):
            for dy in range(NY):
                for dc in range(NC):
                    k = dy * NC + dc
                    if (high, k) == (0, 0):
                        continue
                    row = 2 * ((y + dy) % NY) + flip(c, dc)
                    copy = pltpu.make_async_remote_copy(
                        src_ref=block.at[row],
                        dst_ref=cbuf.at[k, :, 2 * dh + high],
                        send_sem=c_send.at[dh, k, high],
                        recv_sem=c_recv.at[dh, k, high],
                        device_id=near(dy, dc, high, 0),
                        device_id_type=MESH,
                    )
                    copy.start()
                    copies.append(copy)
        cbuf[0, :, 2 * dh, :, :] = block[2 * y + c]
        return copies

    passed = {0: spread(csend, 0)}

    for dy in range(NY):
        for low in range(2):
            k = dy * NC * 2 + low
            if k:
                sino[k].wait_recv()
                share(sbuf.at[k], dy, 1, low, sibling)

    over.wait_recv()
    passed[1] = spread(hbuf, 1)

    for dy in range(NY):
        for low in range(2):
            sino[(dy * NC + 1) * 2 + low].wait_recv()

    def filter_half(part, carry):
        lhs = sbuf[pl.ds(part * 8, 8)].reshape(128, 1024)
        for n in range(4):
            total = None
            for m in range(4):
                at = 768 - 256 * m + 256 * n
                term = jnp.dot(
                    lhs[:, 256 * m : 256 * (m + 1)], g_ref[:, at : at + 256],
                    preferred_element_type=jnp.float32,
                )
                total = term if total is None else total + term
            at = pl.multiple_of(part * 128, 128)
            f_ref[2 * n, pl.ds(at, 128)] = total[:, :128]
            f_ref[2 * n + 1, pl.ds(at, 128)] = total[:, 128:]
        return carry

    lax.fori_loop(0, 2, filter_half, 0)

    def lay_out(k, carry):
        for a in range(2):
            wide = []
            for low in range(2):
                rows = pl.ds((2 * k + low) * 16 + a, 8, stride=2)
                wide.append([f_ref[n, rows, :] for n in range(8)])
            for n in range(NB):
                block = []
                for parts in wide:
                    if n == 0:
                        block.append(parts[0])
                        continue
                    pair = [parts[n - 1], parts[n] if n < 8 else jnp.zeros_like(parts[0])]
                    turned = [pltpu.roll(part, n, 1) for part in pair]
                    lane = lax.broadcasted_iota(jnp.int32, (8, 128), 1)
                    block.append(jnp.where(lane < n, turned[0], turned[1]))
                v_ref[k, a, 16 * n : 16 * (n + 1), :] = jnp.concatenate(block).astype(jnp.bfloat16)
        return carry

    lax.fori_loop(0, NK, lay_out, 0)

    bins = lax.broadcasted_iota(jnp.int32, (128, 256), 0).astype(jnp.float32).astype(jnp.bfloat16)
    own = z * NC + c
    sent = []
    for dh in range(NH):
        for copy in passed[dh]:
            copy.wait_recv()

        def source(k, sums, dh=dh):
            sums = list(sums)
            for a in range(2):
                values = v_ref[k, a]
                for high in range(2):
                    for q in range(2):
                        coord = [
                            jnp.broadcast_to(cbuf[k, a, 2 * dh + high, p : p + 1, :], (8, 128))
                            for p in (2 * q, 2 * q + 1)
                        ]
                        taps = interpolate(values, jnp.concatenate(coord, axis=1), bins)
                        for low in range(2):
                            at = (high * 2 + q) * 2 + low
                            sums[at] = sums[at] + taps[low]
            return tuple(sums)

        zero = jnp.zeros((8, 256), jnp.float32)
        sums = lax.fori_loop(0, NK, source, (zero,) * 8)
        for high in range(2):
            for low in range(2):
                slot = (dh * 2 + high) * 2 + low
                for q in range(2):
                    part = sums[(high * 2 + q) * 2 + low]
                    obuf[slot, :, 256 * q : 256 * (q + 1)] = part.astype(jnp.bfloat16)
                copy = pltpu.make_async_remote_copy(
                    src_ref=obuf.at[slot],
                    dst_ref=o_ref.at[own],
                    send_sem=o_send.at[slot],
                    recv_sem=o_recv.at[own],
                    device_id=owners[slot],
                    device_id_type=MESH,
                )
                mine = jnp.logical_and(owners[slot][0] == ang, owners[slot][1] == sl)
                keep = pltpu.make_async_copy(obuf.at[slot], o_ref.at[own], own_sem)

                @pl.when(jnp.logical_not(mine))
                def _():
                    copy.start()

                @pl.when(mine)
                def _():
                    keep.start()

                sent.append((copy, keep, mine))

    for copy in [over, *sino.values(), *passed[0], *passed[1]]:
        copy.wait_send()

    for copy, keep, mine in sent:

        @pl.when(jnp.logical_not(mine))
        def _():
            copy.wait_send()

        @pl.when(mine)
        def _():
            keep.wait()

    for at, other in enumerate(sources):
        arrival = pltpu.make_async_remote_copy(
            src_ref=obuf.at[0],
            dst_ref=o_ref.at[at],
            send_sem=o_send.at[0],
            recv_sem=o_recv.at[at],
            device_id=other,
            device_id_type=MESH,
        )

        @pl.when(jnp.logical_or(other[0] != ang, other[1] != sl))
        def _():
            arrival.wait_recv()


def shards(sinogram, detector_coord):
    dma = pltpu.SemaphoreType.DMA
    vmem = pl.BlockSpec(memory_space=pltpu.VMEM)
    partials = pl.pallas_call(
        kernel,
        out_shape=jax.ShapeDtypeStruct((NZ * NC, 8, 512), jnp.bfloat16),
        in_specs=[vmem, vmem],
        out_specs=pl.BlockSpec(memory_space=pl.ANY),
        scratch_shapes=[
            pltpu.VMEM((8, 2, 4, 128), jnp.int32),
            pltpu.VMEM((8, 2, 4, 128), jnp.int32),
            pltpu.VMEM((2 * NK, 8, 2, 1024), jnp.bfloat16),
            pltpu.VMEM((NK, 2, 4, 4, 128), jnp.int32),
            pltpu.VMEM((256, 1792), jnp.bfloat16),
            pltpu.VMEM((8, 2 * NK * 16, 128), jnp.float32),
            pltpu.VMEM((NK, 2, NB * 16, 128), jnp.bfloat16),
            pltpu.VMEM((8, 8, 512), jnp.bfloat16),
            dma((2 * NK,)), dma((2 * NK,)),
            dma(()), dma(()),
            dma((NH, NK, 2)), dma((NH, NK, 2)),
            dma((8,)), dma((8,)),
            dma(()),
            pltpu.SemaphoreType.REGULAR((2,)),
        ],
        compiler_params=pltpu.CompilerParams(collective_id=0, has_side_effects=True),
    )(sinogram, detector_coord)
    partials = partials.reshape(NZ, NC, 8, 512).astype(jnp.float32)
    return jnp.sum(partials, axis=0) * jnp.float32(math.pi / 64)


def solution(mesh):
    in_specs = (P("sl", "ang", None), P("ang", "sl", None))
    out_specs = P("ang", "sl", None)
    return jax.shard_map(shards, mesh=mesh, in_specs=in_specs, out_specs=out_specs, check_vma=False)
```

time: 154 us -> 31.6 us (0.21)
  the two profiles are of different devices: /device:TPU:1 before, /device:TPU:25 now
where the time goes in v3:
time: 31.6 us; the launch traced here: 31.3 us
  Pallas kernels  29.8 us (94%)
  other arithmetic  1.48 us (5%)
    pallas_call x1, Pallas kernels, shards(): pl.pallas_call(kernel, out_shape=jax.ShapeDtypeStruct((NZ * NC, 8, 512),...  29.8 us
    reduce_sum x1, other arithmetic, shards(): return jnp.sum(partials, axis=0) * jnp.float32(math.pi / 64)  0.86 us

profile of v3, /device:TPU:25, one launch (start us, length us, event | category | flops | bytes accessed | tf_op | source)
XLA Modules:
  0.0 31.3 jit_solution(16093617312977000856)
XLA Ops:
  0.0 29.8 %shard_map.28 = bf16[8,8,512]{2,1,0:T(8,128)(2,1)} custom-call(bf16[8,2,1024]{2,1,0:T(2,128)(2,1)} %x_ref.1, s32[2,8,512]{2,1,0:T(8,128)} %c_ref.1), custom_call_target="tpu_custom_call" | custom-call | tf_op jit(solution)/shard_map/pallas_call | solution.py:298
  29.8 0.9 %convert_reduce_fusion = f32[2,8,512]{2,1,0:T(8,128)S(1)} fusion(bf16[4,2,8,512]{3,2,1,0:T(8,128)(2,1)} %bitcast.2), kind=kLoop, calls=%fused_computation | loop fusion | flops 57344 | bytes 98304 | tf_op jit(solution)/shard_map/reduce_sum | solution.py:322
  30.7 0.6 %broadcast_multiply_fusion = f32[2,8,512]{2,1,0:T(8,128)} fusion(f32[2,8,512]{2,1,0:T(8,128)S(1)} %convert_reduce_fusion), kind=kLoop, calls=%fused_computation.1 | loop fusion | flops 8192 | bytes 65536 | tf_op jit(solution)/shard_map/mul | solution.py:322

commit v4 on v3

v4 whole, which is shorter than its diff:
```python
import math

import jax
import jax.numpy as jnp
from jax import lax
from jax.experimental import pallas as pl
from jax.experimental.pallas import tpu as pltpu
from jax.sharding import PartitionSpec as P

MESH = pl.DeviceIdType.MESH
NY, NZ, NC, NH, NX = 4, 4, 2, 2, 4
NB, STEP = 9, 127


def flip(bit, by):
    return bit + by - 2 * bit * by


def write_ramp(g_ref):
    depth, width = g_ref.shape

    def chunk(step, carry):
        base = pl.multiple_of(step * 16, 16)
        for lane in range(0, width, 256):
            row = lax.broadcasted_iota(jnp.int32, (16, 256), 0) + base
            column = lax.broadcasted_iota(jnp.int32, (16, 256), 1) + (lane - 768)
            offset = column - row
            real = offset.astype(jnp.float32)
            square = jnp.maximum(real * real, jnp.float32(1.0))
            odd = (offset & 1) != 0
            value = jnp.where(odd, jnp.float32(-1.0 / math.pi**2) / square, jnp.float32(0.0))
            value = jnp.where(offset == 0, jnp.float32(0.25), value)
            g_ref[pl.ds(base, 16), lane : lane + 256] = value.astype(jnp.bfloat16)
        return carry

    lax.fori_loop(0, depth // 16, chunk, 0)


def interpolate(block_values, coord, bins):
    left = coord >> 20
    fraction = (coord & 0xFFFFF).astype(jnp.float32) * jnp.float32(1.0 / 1048576.0)
    block = (left * 8257) >> 20
    within = (left - block * STEP).astype(jnp.float32)

    def rows(value):
        pair = jnp.concatenate([value, value], axis=0).astype(jnp.bfloat16)
        return jnp.concatenate([pair] * 8, axis=0)

    right = jnp.where(bins == rows(within + 1.0), rows(fraction), jnp.zeros((), jnp.bfloat16))
    weights = jnp.where(bins == rows(within), rows(1.0 - fraction), right)
    product = jnp.dot(block_values, weights, preferred_element_type=jnp.float32)
    low, high = product[0:8], product[8:16]
    for n in range(1, NB):
        here = block == n
        low = jnp.where(here, product[16 * n : 16 * n + 8], low)
        high = jnp.where(here, product[16 * n + 8 : 16 * n + 16], high)
    return low, high


def kernel(
    x_ref, c_ref, o_ref,
    cin, csend, hbuf, sbuf, cbuf, g_ref, f_ref, v_ref, obuf,
    in_sem, s_send, s_recv, h_send, h_recv, c_send, c_recv, o_send, o_recv, own_sem, tokens,
):
    load_x = pltpu.make_async_copy(x_ref, sbuf.at[0], in_sem.at[0])
    load_c = pltpu.make_async_copy(c_ref, cin, in_sem.at[1])
    load_x.start()
    load_c.start()
    ang, sl = lax.axis_index("ang"), lax.axis_index("sl")
    y, z, c = ang // 8, (ang // 2) % 4, ang % 2
    h, x = sl // 4, sl % 4
    x_high, x_low = x // 2, x % 2

    def device(yy, zz, cc, hh, xx):
        return (yy * 8 + zz * 2 + cc, hh * 4 + xx)

    def x_at(flip_high, flip_low):
        return flip(x_high, flip_high) * 2 + flip(x_low, flip_low)

    def near(dy, high, low):
        return device((y + dy) % NY, z, c, h, x_at(high, low))

    across = device(y, z, c, flip(h, 1), x)
    sibling = device(y, z, flip(c, 1), h, x)
    far_twin = near(0, 1, 0)
    sharers = [(dy, low) for dy in range(NY) for low in range(2)][1:]
    owners = []
    for dh in range(NH):
        for high in range(2):
            block = flip(h, dh) * NX + x_at(high, 0)
            for low in range(2):
                owners.append((4 * block + y, h * 4 + x_at(0, low)))
    row_x_low = (ang // 4) % 2
    source_sl = h * 4 + 2 * x_high + row_x_low
    sources = [((ang % 4) * 8 + zz * 2 + cc, source_sl) for zz in range(NZ) for cc in range(NC)]

    barrier = pltpu.get_barrier_semaphore()
    group = [across, far_twin, sibling] + [near(dy, 0, low) for dy, low in sharers]
    group += [device(y, (z + dz) % NZ, c, h, x) for dz in range(1, NZ)]
    for other in group:
        pl.semaphore_signal(barrier, inc=1, device_id=other, device_id_type=MESH)
    load_c.wait()
    for a in range(2):
        for p in range(4):
            csend[:, a, p, :] = cin[a, :, 128 * p : 128 * (p + 1)]
    load_x.wait()
    pl.semaphore_wait(barrier, len(group))

    over = pltpu.make_async_remote_copy(
        src_ref=csend, dst_ref=hbuf, send_sem=h_send, recv_sem=h_recv,
        device_id=across, device_id_type=MESH,
    )
    over.start()

    sino = []
    for dy, low in sharers:
        k = dy * 2 + low
        copy = pltpu.make_async_remote_copy(
            src_ref=sbuf.at[0],
            dst_ref=sbuf.at[k],
            send_sem=s_send.at[k],
            recv_sem=s_recv.at[k],
            device_id=near(dy, 0, low),
            device_id_type=MESH,
        )
        copy.start()
        sino.append(copy)
    pl.semaphore_signal(tokens.at[0], inc=1, device_id=far_twin, device_id_type=MESH)
    write_ramp(g_ref)
    pl.semaphore_wait(tokens.at[0], 1)

    def spread(block, dh):
        copies = []
        for high in range(2):
            for dy in range(NY):
                rows = pl.ds(2 * ((y + dy) % NY), 2)
                if (high, dy) == (0, 0):
                    cbuf[0, 2 * dh] = block[rows]
                    continue
                copy = pltpu.make_async_remote_copy(
                    src_ref=block.at[rows],
                    dst_ref=cbuf.at[dy, 2 * dh + high],
                    send_sem=c_send.at[dh, dy, high],
                    recv_sem=c_recv.at[dh, dy, high],
                    device_id=near(dy, high, 0),
                    device_id_type=MESH,
                )
                copy.start()
                copies.append(copy)
        return copies

    passed = {0: spread(csend, 0)}
    over.wait_recv()
    passed[1] = spread(hbuf, 1)
    for copy in sino:
        copy.wait_recv()
    pl.semaphore_signal(tokens.at[1], inc=1, device_id=sibling, device_id_type=MESH)

    lhs = sbuf[...].reshape(128, 1024)
    for n in range(4):
        total = None
        for m in range(4):
            at = 768 - 256 * m + 256 * n
            term = jnp.dot(
                lhs[:, 256 * m : 256 * (m + 1)], g_ref[:, at : at + 256],
                preferred_element_type=jnp.float32,
            )
            total = term if total is None else total + term
        f_ref[2 * n] = total[:, :128]
        f_ref[2 * n + 1] = total[:, 128:]

    def lay_out(k, carry):
        for a in range(2):
            wide = []
            for low in range(2):
                rows = pl.ds((2 * k + low) * 16 + a, 8, stride=2)
                wide.append([f_ref[n, rows, :] for n in range(8)])
            for n in range(NB):
                block = []
                for parts in wide:
                    if n == 0:
                        block.append(parts[0])
                        continue
                    pair = [parts[n - 1], parts[n] if n < 8 else jnp.zeros_like(parts[0])]
                    turned = [pltpu.roll(part, n, 1) for part in pair]
                    lane = lax.broadcasted_iota(jnp.int32, (8, 128), 1)
                    block.append(jnp.where(lane < n, turned[0], turned[1]))
                v_ref[k, a, 16 * n : 16 * (n + 1), :] = jnp.concatenate(block).astype(jnp.bfloat16)
        return carry

    lax.fori_loop(0, NY, lay_out, 0)

    bins = lax.broadcasted_iota(jnp.int32, (128, 256), 0).astype(jnp.float32).astype(jnp.bfloat16)
    own = z * NC + c
    sent = []
    for dh in range(NH):
        for copy in passed[dh]:
            copy.wait_recv()
        for high in range(2):
            sums = {}
            for dy in range(NY):
                for a in range(2):
                    values = v_ref[dy, a]
                    for row in range(2):
                        for q in range(2):
                            coord = [
                                jnp.broadcast_to(
                                    cbuf[dy, 2 * dh + high, row, a, p : p + 1, :], (8, 128)
                                )
                                for p in (2 * q, 2 * q + 1)
                            ]
                            taps = interpolate(values, jnp.concatenate(coord, axis=1), bins)
                            for low in range(2):
                                at = (row, q, low)
                                sums[at] = sums[at] + taps[low] if at in sums else taps[low]
            if (dh, high) == (0, 0):
                pl.semaphore_wait(tokens.at[1], 1)
            for low in range(2):
                slot = (dh * 2 + high) * 2 + low
                for row in range(2):
                    for q in range(2):
                        part = sums[row, q, low].astype(jnp.bfloat16)
                        obuf[slot, row, :, 256 * q : 256 * (q + 1)] = part
                copy = pltpu.make_async_remote_copy(
                    src_ref=obuf.at[slot],
                    dst_ref=o_ref.at[own],
                    send_sem=o_send.at[slot],
                    recv_sem=o_recv.at[own],
                    device_id=owners[slot],
                    device_id_type=MESH,
                )
                mine = jnp.logical_and(owners[slot][0] == ang, owners[slot][1] == sl)
                keep = pltpu.make_async_copy(obuf.at[slot], o_ref.at[own], own_sem)

                @pl.when(jnp.logical_not(mine))
                def _():
                    copy.start()

                @pl.when(mine)
                def _():
                    keep.start()

                sent.append((copy, keep, mine))

    for copy in [over, *sino, *passed[0], *passed[1]]:
        copy.wait_send()

    for copy, keep, mine in sent:

        @pl.when(jnp.logical_not(mine))
        def _():
            copy.wait_send()

        @pl.when(mine)
        def _():
            keep.wait()

    for at, other in enumerate(sources):
        arrival = pltpu.make_async_remote_copy(
            src_ref=obuf.at[0],
            dst_ref=o_ref.at[at],
            send_sem=o_send.at[0],
            recv_sem=o_recv.at[at],
            device_id=other,
            device_id_type=MESH,
        )

        @pl.when(jnp.logical_or(other[0] != ang, other[1] != sl))
        def _():
            arrival.wait_recv()


def shards(sinogram, detector_coord):
    dma = pltpu.SemaphoreType.DMA
    anywhere = pl.BlockSpec(memory_space=pl.ANY)
    partials = pl.pallas_call(
        kernel,
        out_shape=jax.ShapeDtypeStruct((NZ * NC, 2, 8, 512), jnp.bfloat16),
        in_specs=[anywhere, anywhere],
        out_specs=anywhere,
        scratch_shapes=[
            pltpu.VMEM((2, 8, 512), jnp.int32),
            pltpu.VMEM((8, 2, 4, 128), jnp.int32),
            pltpu.VMEM((8, 2, 4, 128), jnp.int32),
            pltpu.VMEM((2 * NY, 8, 2, 1024), jnp.bfloat16),
            pltpu.VMEM((NY, 4, 2, 2, 4, 128), jnp.int32),
            pltpu.VMEM((256, 1792), jnp.bfloat16),
            pltpu.VMEM((8, 128, 128), jnp.float32),
            pltpu.VMEM((NY, 2, NB * 16, 128), jnp.bfloat16),
            pltpu.VMEM((8, 2, 8, 512), jnp.bfloat16),
            dma((2,)),
            dma((2 * NY,)), dma((2 * NY,)),
            dma(()), dma(()),
            dma((NH, NY, 2)), dma((NH, NY, 2)),
            dma((8,)), dma((8,)),
            dma(()),
            pltpu.SemaphoreType.REGULAR((2,)),
        ],
        compiler_params=pltpu.CompilerParams(collective_id=0, has_side_effects=True),
    )(sinogram, detector_coord)
    total = partials[0].astype(jnp.float32)
    for part in range(1, NZ * NC):
        total = total + partials[part].astype(jnp.float32)
    return total * jnp.float32(math.pi / 64)


def solution(mesh):
    in_specs = (P("sl", "ang", None), P("ang", "sl", None))
    out_specs = P("ang", "sl", None)
    return jax.shard_map(shards, mesh=mesh, in_specs=in_specs, out_specs=out_specs, check_vma=False)
```

time: 31.6 us -> 28.7 us (0.908)
  Pallas kernels: 29.8 us -> 26.9 us
    pallas_call x1, Pallas kernels: 29.8 us -> 26.9 us  [shards(): pl.pallas_call(kernel, out_shape=jax.ShapeDtypeStruct((NZ * NC, 2, 8, 512...]
    mul x1, other arithmetic: 0.62 us -> 1.48 us  [shards(): return total * jnp.float32(math.pi / 64)]
    reduce_sum x1 -> x0, other arithmetic: 0.86 us -> none  [shards(): return jnp.sum(partials, axis=0) * jnp.float32(math.pi / 64)]
where the time goes in v4:
time: 28.7 us; the launch traced here: 28.3 us
  Pallas kernels  26.9 us (94%)
  other arithmetic  1.48 us (5%)
    pallas_call x1, Pallas kernels, shards(): pl.pallas_call(kernel, out_shape=jax.ShapeDtypeStruct((NZ * NC, 2, 8, 512...  26.9 us
    mul x1, other arithmetic, shards(): return total * jnp.float32(math.pi / 64)  1.48 us

profile of v4, /device:TPU:25, one launch (start us, length us, event | category | flops | bytes accessed | tf_op | source)
XLA Modules:
  0.0 28.3 jit_solution(16946155353214057944)
XLA Ops:
  0.0 26.9 %shard_map.28 = bf16[8,2,8,512]{3,2,1,0:T(8,128)(2,1)} custom-call(bf16[8,2,1024]{2,1,0:T(2,128)(2,1)} %x_ref.1, s32[2,8,512]{2,1,0:T(8,128)} %c_ref.1), custom_call_target="tpu_custom_call" | custom-call | tf_op jit(solution)/shard_map/pallas_call | solution.py:276
  26.9 1.5 %multiply_bitcast_fusion = f32[2,8,512]{2,1,0:T(8,128)} fusion(bf16[8,2,8,512]{3,2,1,0:T(8,128)(2,1)} %shard_map.28), kind=kLoop, calls=%fused_computation | loop fusion | flops 131072 | bytes 163840 | tf_op jit(solution)/shard_map/mul | solution.py:304

commit v5 on v4

--- a/solution.py
+++ b/solution.py
@@ -82,17 +82,22 @@
 
     across = device(y, z, c, flip(h, 1), x)
     sibling = device(y, z, flip(c, 1), h, x)
-    far_twin = near(0, 1, 0)
+    far_twin = near(0, 1, 1)
     sharers = [(dy, low) for dy in range(NY) for low in range(2)][1:]
+    def pair_of(yy, hh):
+        return (yy + 2 * hh) % NY
+
     owners = []
     for dh in range(NH):
-        for high in range(2):
-            block = flip(h, dh) * NX + x_at(high, 0)
+        for far in range(2):
+            h_block = flip(h, dh)
+            block = h_block * NX + x_at(far, far)
             for low in range(2):
-                owners.append((4 * block + y, h * 4 + x_at(0, low)))
-    row_x_low = (ang // 4) % 2
-    source_sl = h * 4 + 2 * x_high + row_x_low
-    sources = [((ang % 4) * 8 + zz * 2 + cc, source_sl) for zz in range(NZ) for cc in range(NC)]
+                owners.append((4 * block + pair_of(y, h_block), h * 4 + x_at(0, low)))
+    h_row, x_row = ang // 16, (ang // 4) % 4
+    source_sl = h * 4 + 2 * x_high + flip(x_row % 2, flip(x_row // 2, x_high))
+    source_y = pair_of(ang % 4, h_row)
+    sources = [(source_y * 8 + zz * 2 + cc, source_sl) for zz in range(NZ) for cc in range(NC)]
 
     barrier = pltpu.get_barrier_semaphore()
     group = [across, far_twin, sibling] + [near(dy, 0, low) for dy, low in sharers]
@@ -133,7 +138,7 @@
         copies = []
         for high in range(2):
             for dy in range(NY):
-                rows = pl.ds(2 * ((y + dy) % NY), 2)
+                rows = pl.ds(2 * pair_of(y + dy, flip(h, dh)), 2)
                 if (high, dy) == (0, 0):
                     cbuf[0, 2 * dh] = block[rows]
                     continue
@@ -142,7 +147,7 @@
                     dst_ref=cbuf.at[dy, 2 * dh + high],
                     send_sem=c_send.at[dh, dy, high],
                     recv_sem=c_recv.at[dh, dy, high],
-                    device_id=near(dy, high, 0),
+                    device_id=near(dy, high, high),
                     device_id_type=MESH,
                 )
                 copy.start()

time: 28.7 us -> 25.2 us (0.88)
  Pallas kernels: 26.9 us -> 23.5 us
    pallas_call x1, Pallas kernels: 26.9 us -> 23.5 us  [shards(): pl.pallas_call(kernel, out_shape=jax.ShapeDtypeStruct((NZ * NC, 2, 8, 512...]
where the time goes in v5:
time: 25.2 us; the launch traced here: 25 us
  Pallas kernels  23.5 us (93%)
  other arithmetic  1.48 us (6%)
    pallas_call x1, Pallas kernels, shards(): pl.pallas_call(kernel, out_shape=jax.ShapeDtypeStruct((NZ * NC, 2, 8, 512...  23.5 us
    mul x1, other arithmetic, shards(): return total * jnp.float32(math.pi / 64)  1.48 us

profile of v5, /device:TPU:25, one launch (start us, length us, event | category | flops | bytes accessed | tf_op | source)
XLA Modules:
  0.0 25.0 jit_solution(4879052338108913204)
XLA Ops:
  0.0 23.5 %shard_map.28 = bf16[8,2,8,512]{3,2,1,0:T(8,128)(2,1)} custom-call(bf16[8,2,1024]{2,1,0:T(2,128)(2,1)} %x_ref.1, s32[2,8,512]{2,1,0:T(8,128)} %c_ref.1), custom_call_target="tpu_custom_call" | custom-call | tf_op jit(solution)/shard_map/pallas_call | solution.py:281
  23.5 1.5 %multiply_bitcast_fusion = f32[2,8,512]{2,1,0:T(8,128)} fusion(bf16[8,2,8,512]{3,2,1,0:T(8,128)(2,1)} %shard_map.28), kind=kLoop, calls=%fused_computation | loop fusion | flops 131072 | bytes 163840 | tf_op jit(solution)/shard_map/mul | solution.py:309

commit v6 on v5

--- a/solution.py
+++ b/solution.py
@@ -135,23 +135,23 @@
     pl.semaphore_wait(tokens.at[0], 1)
 
     def spread(block, dh):
-        copies = []
-        for high in range(2):
+        copies = {}
+        for far in range(2):
             for dy in range(NY):
                 rows = pl.ds(2 * pair_of(y + dy, flip(h, dh)), 2)
-                if (high, dy) == (0, 0):
+                if (far, dy) == (0, 0):
                     cbuf[0, 2 * dh] = block[rows]
                     continue
                 copy = pltpu.make_async_remote_copy(
                     src_ref=block.at[rows],
-                    dst_ref=cbuf.at[dy, 2 * dh + high],
-                    send_sem=c_send.at[dh, dy, high],
-                    recv_sem=c_recv.at[dh, dy, high],
-                    device_id=near(dy, high, high),
+                    dst_ref=cbuf.at[dy, 2 * dh + far],
+                    send_sem=c_send.at[dh, dy, far],
+                    recv_sem=c_recv.at[dh, dy, far],
+                    device_id=near(dy, far, far),
                     device_id_type=MESH,
                 )
                 copy.start()
-                copies.append(copy)
+                copies[far, dy] = copy
         return copies
 
     passed = {0: spread(csend, 0)}
@@ -199,9 +199,10 @@
     own = z * NC + c
     sent = []
     for dh in range(NH):
-        for copy in passed[dh]:
-            copy.wait_recv()
         for high in range(2):
+            for dy in range(NY):
+                if (high, dy) in passed[dh]:
+                    passed[dh][high, dy].wait_recv()
             sums = {}
             for dy in range(NY):
                 for a in range(2):
@@ -222,10 +223,10 @@
                 pl.semaphore_wait(tokens.at[1], 1)
             for low in range(2):
                 slot = (dh * 2 + high) * 2 + low
-                for row in range(2):
-                    for q in range(2):
-                        part = sums[row, q, low].astype(jnp.bfloat16)
-                        obuf[slot, row, :, 256 * q : 256 * (q + 1)] = part
+                for q in range(2):
+                    both = jnp.concatenate([sums[0, q, low], sums[1, q, low]], axis=0)
+                    both = (both * jnp.float32(math.pi / 64)).astype(jnp.bfloat16)
+                    obuf[slot, :, 256 * q : 256 * (q + 1)] = both
                 copy = pltpu.make_async_remote_copy(
                     src_ref=obuf.at[slot],
                     dst_ref=o_ref.at[own],
@@ -247,7 +248,7 @@
 
                 sent.append((copy, keep, mine))
 
-    for copy in [over, *sino, *passed[0], *passed[1]]:
+    for copy in [over, *sino, *passed[0].values(), *passed[1].values()]:
         copy.wait_send()
 
     for copy, keep, mine in sent:
@@ -280,7 +281,7 @@
     anywhere = pl.BlockSpec(memory_space=pl.ANY)
     partials = pl.pallas_call(
         kernel,
-        out_shape=jax.ShapeDtypeStruct((NZ * NC, 2, 8, 512), jnp.bfloat16),
+        out_shape=jax.ShapeDtypeStruct((NZ * NC, 16, 512), jnp.bfloat16),
         in_specs=[anywhere, anywhere],
         out_specs=anywhere,
         scratch_shapes=[
@@ -292,7 +293,7 @@
             pltpu.VMEM((256, 1792), jnp.bfloat16),
             pltpu.VMEM((8, 128, 128), jnp.float32),
             pltpu.VMEM((NY, 2, NB * 16, 128), jnp.bfloat16),
-            pltpu.VMEM((8, 2, 8, 512), jnp.bfloat16),
+            pltpu.VMEM((8, 16, 512), jnp.bfloat16),
             dma((2,)),
             dma((2 * NY,)), dma((2 * NY,)),
             dma(()), dma(()),
@@ -303,10 +304,7 @@
         ],
         compiler_params=pltpu.CompilerParams(collective_id=0, has_side_effects=True),
     )(sinogram, detector_coord)
-    total = partials[0].astype(jnp.float32)
-    for part in range(1, NZ * NC):
-        total = total + partials[part].astype(jnp.float32)
-    return total * jnp.float32(math.pi / 64)
+    return jnp.sum(partials.astype(jnp.float32), axis=0).reshape(2, 8, 512)
 
 
 def solution(mesh):

time: 25.2 us -> 24.3 us (0.964)
  Pallas kernels: 23.5 us -> 22.6 us
    reduce_sum x0 -> x1, other arithmetic: none -> 1.54 us  [shards(): return jnp.sum(partials.astype(jnp.float32), axis=0).reshape(2, 8, 512)]
    mul x1 -> x0, other arithmetic: 1.48 us -> none  [shards(): return total * jnp.float32(math.pi / 64)]
    pallas_call x1, Pallas kernels: 23.5 us -> 22.6 us  [shards(): pl.pallas_call(kernel, out_shape=jax.ShapeDtypeStruct((NZ * NC, 16, 512),...]
where the time goes in v6:
time: 24.3 us; the launch traced here: 24.2 us
  Pallas kernels  22.6 us (93%)
  other arithmetic  1.54 us (6%)
    pallas_call x1, Pallas kernels, shards(): pl.pallas_call(kernel, out_shape=jax.ShapeDtypeStruct((NZ * NC, 16, 512),...  22.6 us
    reduce_sum x1, other arithmetic, shards(): return jnp.sum(partials.astype(jnp.float32), axis=0).reshape(2, 8, 512)  1.54 us

profile of v6, /device:TPU:25, one launch (start us, length us, event | category | flops | bytes accessed | tf_op | source)
XLA Modules:
  0.0 24.2 jit_solution(3408244748453377362)
XLA Ops:
  0.0 22.6 %shard_map.28 = bf16[8,16,512]{2,1,0:T(8,128)(2,1)} custom-call(bf16[8,2,1024]{2,1,0:T(2,128)(2,1)} %x_ref.1, s32[2,8,512]{2,1,0:T(8,128)} %c_ref.1), custom_call_target="tpu_custom_call" | custom-call | tf_op jit(solution)/shard_map/pallas_call | solution.py:282
  22.6 1.5 %convert_reduce_fusion = f32[16,512]{1,0:T(8,128)} fusion(bf16[8,16,512]{2,1,0:T(8,128)(2,1)} %shard_map.28), kind=kLoop, calls=%fused_computation | loop fusion | flops 122880 | bytes 163840 | tf_op jit(solution)/shard_map/reduce_sum | solution.py:307

commit v7 on v6

--- a/solution.py
+++ b/solution.py
@@ -281,7 +281,7 @@
     anywhere = pl.BlockSpec(memory_space=pl.ANY)
     partials = pl.pallas_call(
         kernel,
-        out_shape=jax.ShapeDtypeStruct((NZ * NC, 16, 512), jnp.bfloat16),
+        out_shape=pltpu.VMEM((NZ * NC, 16, 512), jnp.bfloat16),
         in_specs=[anywhere, anywhere],
         out_specs=anywhere,
         scratch_shapes=[

time: 24.3 us -> 23.3 us (0.959)
  other arithmetic: 1.54 us -> 0.64 us
    reduce_sum x1, other arithmetic: 1.54 us -> 0.64 us  [shards(): return jnp.sum(partials.astype(jnp.float32), axis=0).reshape(2, 8, 512)]
where the time goes in v7:
time: 23.3 us; the launch traced here: 23.1 us
  Pallas kernels  22.5 us (97%)
  other arithmetic  0.64 us (3%)
    pallas_call x1, Pallas kernels, shards(): pl.pallas_call(kernel, out_shape=pltpu.VMEM((NZ * NC, 16, 512), jnp.bfloa...  22.5 us
    reduce_sum x1, other arithmetic, shards(): return jnp.sum(partials.astype(jnp.float32), axis=0).reshape(2, 8, 512)  0.64 us

profile of v7, /device:TPU:25, one launch (start us, length us, event | category | flops | bytes accessed | tf_op | source)
XLA Modules:
  0.0 23.1 jit_solution(11077196391264978440)
XLA Ops:
  0.0 22.5 %shard_map.28 = bf16[8,16,512]{2,1,0:T(8,128)(2,1)S(1)} custom-call(bf16[8,2,1024]{2,1,0:T(2,128)(2,1)} %x_ref.1, s32[2,8,512]{2,1,0:T(8,128)} %c_ref.1), custom_call_target="tpu_custom_call" | custom-call | tf_op jit(solution)/shard_map/pallas_call | solution.py:282
  22.5 0.6 %convert_reduce_fusion = f32[16,512]{1,0:T(8,128)} fusion(bf16[8,16,512]{2,1,0:T(8,128)(2,1)S(1)} %shard_map.28), kind=kLoop, calls=%fused_computation | loop fusion | flops 122880 | bytes 163840 | tf_op jit(solution)/shard_map/reduce_sum | solution.py:307

commit v8 on v7

--- a/solution.py
+++ b/solution.py
@@ -221,7 +221,7 @@
                                 sums[at] = sums[at] + taps[low] if at in sums else taps[low]
             if (dh, high) == (0, 0):
                 pl.semaphore_wait(tokens.at[1], 1)
-            for low in range(2):
+            for low in (1, 0):
                 slot = (dh * 2 + high) * 2 + low
                 for q in range(2):
                     both = jnp.concatenate([sums[0, q, low], sums[1, q, low]], axis=0)

time: 23.3 us -> 23.1 us (level)
  no operation moved by 1% of the time
where the time goes in v8:
time: 23.1 us; the launch traced here: 23 us
  Pallas kernels  22.3 us (97%)
  other arithmetic  0.64 us (3%)
    pallas_call x1, Pallas kernels, shards(): pl.pallas_call(kernel, out_shape=pltpu.VMEM((NZ * NC, 16, 512), jnp.bfloa...  22.3 us
    reduce_sum x1, other arithmetic, shards(): return jnp.sum(partials.astype(jnp.float32), axis=0).reshape(2, 8, 512)  0.64 us

profile of v8, /device:TPU:25, one launch (start us, length us, event | category | flops | bytes accessed | tf_op | source)
XLA Modules:
  0.0 23.0 jit_solution(3576960431623195435)
XLA Ops:
  0.0 22.3 %shard_map.28 = bf16[8,16,512]{2,1,0:T(8,128)(2,1)S(1)} custom-call(bf16[8,2,1024]{2,1,0:T(2,128)(2,1)} %x_ref.1, s32[2,8,512]{2,1,0:T(8,128)} %c_ref.1), custom_call_target="tpu_custom_call" | custom-call | tf_op jit(solution)/shard_map/pallas_call | solution.py:282
  22.3 0.6 %convert_reduce_fusion = f32[16,512]{1,0:T(8,128)} fusion(bf16[8,16,512]{2,1,0:T(8,128)(2,1)S(1)} %shard_map.28), kind=kLoop, calls=%fused_computation | loop fusion | flops 122880 | bytes 163840 | tf_op jit(solution)/shard_map/reduce_sum | solution.py:307

commit v9 on v8

--- a/solution.py
+++ b/solution.py
@@ -83,7 +83,8 @@
     across = device(y, z, c, flip(h, 1), x)
     sibling = device(y, z, flip(c, 1), h, x)
     far_twin = near(0, 1, 1)
-    sharers = [(dy, low) for dy in range(NY) for low in range(2)][1:]
+    twin = near(0, 0, 1)
+    sharers = [(0, 1), (1, 0), (1, 1), (3, 0), (3, 1), (2, 0), (2, 1)]
     def pair_of(yy, hh):
         return (yy + 2 * hh) % NY
 
@@ -100,7 +101,7 @@
     sources = [(source_y * 8 + zz * 2 + cc, source_sl) for zz in range(NZ) for cc in range(NC)]
 
     barrier = pltpu.get_barrier_semaphore()
-    group = [across, far_twin, sibling] + [near(dy, 0, low) for dy, low in sharers]
+    group = [across, far_twin, sibling] + [near(dy, 0, low) for dy, low in sharers[:-1]]
     group += [device(y, (z + dz) % NZ, c, h, x) for dz in range(1, NZ)]
     for other in group:
         pl.semaphore_signal(barrier, inc=1, device_id=other, device_id_type=MESH)
@@ -118,7 +119,11 @@
     over.start()
 
     sino = []
+    pl.semaphore_signal(tokens.at[0], inc=1, device_id=far_twin, device_id_type=MESH)
+    pl.semaphore_signal(tokens.at[2], inc=1, device_id=twin, device_id_type=MESH)
     for dy, low in sharers:
+        if (dy, low) == sharers[-1]:
+            pl.semaphore_wait(tokens.at[2], 1)
         k = dy * 2 + low
         copy = pltpu.make_async_remote_copy(
             src_ref=sbuf.at[0],
@@ -130,7 +135,6 @@
         )
         copy.start()
         sino.append(copy)
-    pl.semaphore_signal(tokens.at[0], inc=1, device_id=far_twin, device_id_type=MESH)
     write_ramp(g_ref)
     pl.semaphore_wait(tokens.at[0], 1)
 
@@ -300,7 +304,7 @@
             dma((NH, NY, 2)), dma((NH, NY, 2)),
             dma((8,)), dma((8,)),
             dma(()),
-            pltpu.SemaphoreType.REGULAR((2,)),
+            pltpu.SemaphoreType.REGULAR((3,)),
         ],
         compiler_params=pltpu.CompilerParams(collective_id=0, has_side_effects=True),
     )(sinogram, detector_coord)

time: 23.1 us -> 23 us (level)
    pallas_call x1, Pallas kernels: 22.3 us -> 22.1 us  [shards(): pl.pallas_call(kernel, out_shape=pltpu.VMEM((NZ * NC, 16, 512), jnp.bfloa...]
where the time goes in v9:
time: 23 us; the launch traced here: 22.7 us
  Pallas kernels  22.1 us (96%)
  other arithmetic  0.64 us (3%)
    pallas_call x1, Pallas kernels, shards(): pl.pallas_call(kernel, out_shape=pltpu.VMEM((NZ * NC, 16, 512), jnp.bfloa...  22.1 us
    reduce_sum x1, other arithmetic, shards(): return jnp.sum(partials.astype(jnp.float32), axis=0).reshape(2, 8, 512)  0.64 us

profile of v9, /device:TPU:25, one launch (start us, length us, event | category | flops | bytes accessed | tf_op | source)
XLA Modules:
  0.0 22.7 jit_solution(11298610255806738870)
XLA Ops:
  0.0 22.1 %shard_map.28 = bf16[8,16,512]{2,1,0:T(8,128)(2,1)S(1)} custom-call(bf16[8,2,1024]{2,1,0:T(2,128)(2,1)} %x_ref.1, s32[2,8,512]{2,1,0:T(8,128)} %c_ref.1), custom_call_target="tpu_custom_call" | custom-call | tf_op jit(solution)/shard_map/pallas_call | solution.py:286
  22.1 0.6 %convert_reduce_fusion = f32[16,512]{1,0:T(8,128)} fusion(bf16[8,16,512]{2,1,0:T(8,128)(2,1)S(1)} %shard_map.28), kind=kLoop, calls=%fused_computation | loop fusion | flops 122880 | bytes 163840 | tf_op jit(solution)/shard_map/reduce_sum | solution.py:311
